TPU v7x, 32 devices: a whole 2x2x4 slice. The times are simulated.
32 devices in a mesh: seq: 4 (over y, x), fsdp: 8 (over z, core).
Axes of the slice: x: 2, y: 2, z: 4, core: 2. Of those that a mesh axis runs over, the one named last changes fastest.
Arguments:
- block_input: bfloat16 [2, 8, 1024, 2048], P(None, 'fsdp', 'seq'), may hold values from -6 to 6
- out_grad: bfloat16 [2, 8, 1024, 2048], P(None, 'fsdp', 'seq'), may hold values from -6 to 6
- query_proj: bfloat16 [2048, 2048], P('fsdp', 'seq'), may hold values from -0.125 to 0.125
- key_projection: bfloat16 [2048, 1024], P('fsdp', 'seq'), may hold values from -0.125 to 0.125
- value_projection: bfloat16 [2048, 1024], P('fsdp', 'seq'), may hold values from -0.125 to 0.125
- outgate_proj: bfloat16 [2048, 2048], P('fsdp', 'seq'), may hold values from -0.125 to 0.125
- output_proj: bfloat16 [2048, 2048], P('seq', 'fsdp'), may hold values from -1 to 1
- ffgate_proj: bfloat16 [2048, 6144], P('fsdp', 'seq'), may hold values from -0.125 to 0.125
- ffup_proj: bfloat16 [2048, 6144], P('fsdp', 'seq'), may hold values from -0.125 to 0.125
- ffdown_proj: bfloat16 [6144, 2048], P('seq', 'fsdp'), may hold values from -0.078125 to 0.078125
- attn_gain: float32 [2048], replicated, may hold values from 0.5 to 1.5
- ffn_gain: float32 [2048], replicated, may hold values from 0.5 to 1.5
- query_gain: float32 [128], replicated, may hold values from 0.1 to 1.9
- key_gain: float32 [128], replicated, may hold values from 0.1 to 1.9
- piece_order: int32 [2, 8, 8], P(None, 'fsdp'), may hold values from 0 to 7, each once within a row
- doc_ids: int32 [2, 8, 1024], P(None, 'fsdp'), may hold values from 0 to 3, never falling along the last dimension, each value on 1 to 512 neighbouring positions
Outputs:
- block_output: bfloat16 [2, 8, 1024, 2048], P(None, 'fsdp', 'seq')
- input_grad: bfloat16 [2, 8, 1024, 2048], P(None, 'fsdp', 'seq')
- query_grad: float32 [2048, 2048], P('fsdp', 'seq')
- key_grad: float32 [2048, 1024], P('fsdp', 'seq')
- value_grad: float32 [2048, 1024], P('fsdp', 'seq')
- outgate_grad: float32 [2048, 2048], P('fsdp', 'seq')
- output_grad: float32 [2048, 2048], P('seq', 'fsdp')
- ffgate_grad: float32 [2048, 6144], P('fsdp', 'seq')
- ffup_grad: float32 [2048, 6144], P('fsdp', 'seq')
- ffdown_grad: float32 [6144, 2048], P('seq', 'fsdp')
- attn_gain_grad: float32 [2048], replicated
- ffn_gain_grad: float32 [2048], replicated
- query_gain_grad: float32 [128], replicated
- key_gain_grad: float32 [128], replicated
Inputs may be any that keep to these rules, and one draw needn't show every extreme that they name: For each sequence, piece_order is a permutation of the 8 first pieces. `doc_ids`: document numbers never fall along a sequence's first order; each of the 4 documents covers 1 to 512 positions, and one covers exactly 512.
All inputs are finite; a program needn't handle non-finite values.
Results may differ from a plain program's by a relative error of at most 0.02.
Values may be sent and summed in bfloat16 or wider, within the bound.
A program may use at most 320 MiB of HBM per device.

v0:
```python
from functools import partial
import math

import jax
import jax.numpy as jnp
from jax import lax
from jax.sharding import PartitionSpec as P

HEAD_SIZE = 128


EPSILON = 1e-06
ROPE_BASE = 5000000.0
NEG_LARGE = -1e30


def rms_scale(values):
    return lax.rsqrt(jnp.mean(values * values, axis=-1, keepdims=True) + EPSILON)


def rms_back(grad_out, normed, scales, gain):
    scaled_grad = grad_out * gain
    return scales * (scaled_grad - normed * jnp.mean(scaled_grad * normed, axis=-1, keepdims=True))


def rope_tables(positions, head_dim):
    half_dim = head_dim // 2
    inverse = jnp.exp(
        -math.log(ROPE_BASE) * 2.0 * jnp.arange(half_dim, dtype=jnp.float32) / head_dim
    )
    angles = positions.astype(jnp.float32)[:, None] * inverse[None, :]
    cosines = jnp.cos(angles)
    sines = jnp.sin(angles)
    return (jnp.concatenate([cosines, cosines], -1), jnp.concatenate([sines, sines], -1))


def apply_rotary(values, cosine_lookup, sine_lookup):
    half_dim = values.shape[-1] // 2
    turned = jnp.concatenate([-values[..., half_dim:], values[..., :half_dim]], -1)
    return values * cosine_lookup + turned * sine_lookup


def rotate_back(values, cosine_lookup, sine_lookup):
    half_dim = values.shape[-1] // 2
    shifted = values * sine_lookup
    turned = jnp.concatenate([shifted[..., half_dim:], -shifted[..., :half_dim]], -1)
    return values * cosine_lookup + turned


def visible_mask(positions, doc_rows, begin_row, end_row):
    return (positions[None, :] <= positions[begin_row:end_row, None]) & (
        doc_rows[None, :] == doc_rows[begin_row:end_row, None]
    )


def block_scores(query_row_block, key_rows, positions, doc_rows, begin_row, end_row, score_scale):
    scores = (
        jnp.einsum(
            "qhgd,khd->hgqk",
            query_row_block[begin_row:end_row],
            key_rows,
            preferred_element_type=jnp.float32,
        )
        * score_scale
    )
    return jnp.where(visible_mask(positions, doc_rows, begin_row, end_row), scores, NEG_LARGE)


def attend_forward(item, score_scale):
    query_row_block, key_rows, value_row_block, positions, doc_rows = item
    sequence_length = query_row_block.shape[0]
    block_rows = min(512, sequence_length)
    outputs = []
    totals = []
    for begin_row in range(0, sequence_length, block_rows):
        end_row = begin_row + block_rows
        scores = block_scores(
            query_row_block, key_rows, positions, doc_rows, begin_row, end_row, score_scale
        )
        highest = jnp.max(scores, axis=-1, keepdims=True)
        exponents = jnp.exp(scores - highest)
        denominator = jnp.sum(exponents, axis=-1, keepdims=True)
        prob_low = (exponents / denominator).astype(jnp.bfloat16)
        outputs.append(
            jnp.einsum(
                "hgqk,khd->qhgd", prob_low, value_row_block, preferred_element_type=jnp.float32
            )
        )
        totals.append((highest + jnp.log(denominator))[..., 0])
    return (jnp.concatenate(outputs, 0), jnp.concatenate(totals, -1))


def attend_backward(item, score_scale):
    query_row_block, key_rows, value_row_block, out_grads, log_totals, positions, doc_rows = item
    sequence_length = query_row_block.shape[0]
    block_rows = min(512, sequence_length)
    key_sum = jnp.zeros(key_rows.shape, jnp.float32)
    value_sum = jnp.zeros(value_row_block.shape, jnp.float32)
    query_parts = []
    for begin_row in range(0, sequence_length, block_rows):
        end_row = begin_row + block_rows
        scores = block_scores(
            query_row_block, key_rows, positions, doc_rows, begin_row, end_row, score_scale
        )
        probs = jnp.exp(scores - log_totals[..., begin_row:end_row, None])
        prob_grad = jnp.einsum(
            "qhgd,khd->hgqk",
            out_grads[begin_row:end_row],
            value_row_block,
            preferred_element_type=jnp.float32,
        )
        score_grad = (
            probs * (prob_grad - jnp.sum(prob_grad * probs, axis=-1, keepdims=True)) * score_scale
        ).astype(jnp.bfloat16)
        query_parts.append(
            jnp.einsum("hgqk,khd->qhgd", score_grad, key_rows, preferred_element_type=jnp.float32)
        )
        key_sum = key_sum + jnp.einsum(
            "hgqk,qhgd->khd",
            score_grad,
            query_row_block[begin_row:end_row],
            preferred_element_type=jnp.float32,
        )
        value_sum = value_sum + jnp.einsum(
            "hgqk,qhgd->khd",
            probs.astype(jnp.bfloat16),
            out_grads[begin_row:end_row],
            preferred_element_type=jnp.float32,
        )
    return (jnp.concatenate(query_parts, 0), key_sum, value_sum)


def dense(left, right):
    return jnp.dot(left, right, preferred_element_type=jnp.float32)


def shards(
    block_input,
    out_grad,
    query_proj,
    key_projection,
    value_projection,
    outgate_proj,
    output_proj,
    ffgate_proj,
    ffup_proj,
    ffdown_proj,
    attn_gain,
    ffn_gain,
    query_gain,
    key_gain,
    piece_order,
    doc_ids,
):
    seq_devices = lax.axis_size("seq")
    micro_count, seq_count, local_len, feature_dim = block_input.shape
    full_len = local_len * seq_devices
    piece_len = full_len // piece_order.shape[2]
    row_count = seq_count * full_len
    query_heads = query_proj.shape[1] // HEAD_SIZE
    kv_heads = key_projection.shape[1] // HEAD_SIZE
    heads_per_group = query_heads // kv_heads
    score_scale = HEAD_SIZE ** (-0.5)
    weight_list = (
        query_proj,
        key_projection,
        value_projection,
        outgate_proj,
        output_proj,
        ffgate_proj,
        ffup_proj,
        ffdown_proj,
    )
    grad_sums = tuple((jnp.zeros(weight_shard.shape, jnp.float32) for weight_shard in weight_list))
    attn_gain_sum = jnp.zeros((feature_dim,), jnp.float32)
    ffn_gain_sum = jnp.zeros((feature_dim,), jnp.float32)
    query_gain_sum = jnp.zeros((HEAD_SIZE,), jnp.float32)
    key_gain_sum = jnp.zeros((HEAD_SIZE,), jnp.float32)
    outputs = []
    input_grads = []
    for micro_idx in range(micro_count):
        inputs_now = block_input[micro_idx].astype(jnp.float32)
        scale_one = rms_scale(inputs_now)
        first_normalized = inputs_now * scale_one
        attn_rows = lax.all_gather(
            (first_normalized * attn_gain).astype(jnp.bfloat16), "seq", axis=1, tiled=True
        ).reshape(row_count, feature_dim)
        query_full, key_full, value_full, outgate_full, output_full = (
            lax.all_gather(query_proj, "fsdp", axis=0, tiled=True),
            lax.all_gather(key_projection, "fsdp", axis=0, tiled=True),
            lax.all_gather(value_projection, "fsdp", axis=0, tiled=True),
            lax.all_gather(outgate_proj, "fsdp", axis=0, tiled=True),
            lax.all_gather(output_proj, "fsdp", axis=1, tiled=True),
        )
        query_before_rotation = dense(attn_rows, query_full).reshape(
            row_count, query_heads, HEAD_SIZE
        )
        key_before_rotation = dense(attn_rows, key_full).reshape(row_count, kv_heads, HEAD_SIZE)
        value_low = dense(attn_rows, value_full).astype(jnp.bfloat16)
        gate_pre = dense(attn_rows, outgate_full)
        order_now = piece_order[micro_idx]
        positions = (
            order_now[:, :, None] * piece_len
            + jnp.arange(piece_len, dtype=jnp.int32)[None, None, :]
        ).reshape(seq_count, full_len)
        doc_rows = jnp.take_along_axis(doc_ids[micro_idx], positions, axis=1)
        cosine_lookup, sine_lookup = rope_tables(positions.reshape(row_count), HEAD_SIZE)
        cosine_lookup = cosine_lookup[:, None, :]
        sine_lookup = sine_lookup[:, None, :]
        query_scale = rms_scale(query_before_rotation)
        query_normed = query_before_rotation * query_scale
        query_low = apply_rotary(query_normed * query_gain, cosine_lookup, sine_lookup).astype(
            jnp.bfloat16
        )
        key_scale = rms_scale(key_before_rotation)
        key_normed = key_before_rotation * key_scale
        key_low = apply_rotary(key_normed * key_gain, cosine_lookup, sine_lookup).astype(
            jnp.bfloat16
        )
        query_seq = query_low.reshape(seq_count, full_len, kv_heads, heads_per_group, HEAD_SIZE)
        key_seq = key_low.reshape(seq_count, full_len, kv_heads, HEAD_SIZE)
        value_seq = value_low.reshape(seq_count, full_len, kv_heads, HEAD_SIZE)
        attn_out, log_totals = lax.map(
            partial(attend_forward, score_scale=score_scale),
            (query_seq, key_seq, value_seq, positions, doc_rows),
        )
        attn_out = attn_out.reshape(row_count, query_heads * HEAD_SIZE)
        gate_sig = jax.nn.sigmoid(gate_pre)
        gated_low = (attn_out * gate_sig).astype(jnp.bfloat16)
        attn_part = dense(gated_low, output_full).reshape(seq_count, full_len, feature_dim)
        middle = inputs_now + lax.psum_scatter(attn_part, "seq", scatter_dimension=1, tiled=True)
        scale_two = rms_scale(middle)
        normed_two = middle * scale_two
        ffn_rows = lax.all_gather(
            (normed_two * ffn_gain).astype(jnp.bfloat16), "seq", axis=1, tiled=True
        ).reshape(row_count, feature_dim)
        ffgate_full, ffup_full, ffdown_full = (
            lax.all_gather(ffgate_proj, "fsdp", axis=0, tiled=True),
            lax.all_gather(ffup_proj, "fsdp", axis=0, tiled=True),
            lax.all_gather(ffdown_proj, "fsdp", axis=1, tiled=True),
        )
        gate_ffn = dense(ffn_rows, ffgate_full)
        up_ffn = dense(ffn_rows, ffup_full)
        gate_sigm = jax.nn.sigmoid(gate_ffn)
        silu_gate = gate_ffn * gate_sigm
        hidden_low = (silu_gate * up_ffn).astype(jnp.bfloat16)
        ffn_part = dense(hidden_low, ffdown_full).reshape(seq_count, full_len, feature_dim)
        block_out = middle + lax.psum_scatter(
            ffn_part.astype(jnp.bfloat16), "seq", scatter_dimension=1, tiled=True
        ).astype(jnp.float32)
        outputs.append(block_out.astype(jnp.bfloat16))
        (
            query_back,
            key_back,
            value_back,
            outgate_back,
            output_back,
            ffgate_back,
            ffup_back,
            ffdown_back,
        ) = (
            lax.all_gather(query_proj, "fsdp", axis=0, tiled=True),
            lax.all_gather(key_projection, "fsdp", axis=0, tiled=True),
            lax.all_gather(value_projection, "fsdp", axis=0, tiled=True),
            lax.all_gather(outgate_proj, "fsdp", axis=0, tiled=True),
            lax.all_gather(output_proj, "fsdp", axis=1, tiled=True),
            lax.all_gather(ffgate_proj, "fsdp", axis=0, tiled=True),
            lax.all_gather(ffup_proj, "fsdp", axis=0, tiled=True),
            lax.all_gather(ffdown_proj, "fsdp", axis=1, tiled=True),
        )
        cot_now = out_grad[micro_idx]
        cot_rows = lax.all_gather(cot_now, "seq", axis=1, tiled=True).reshape(
            row_count, feature_dim
        )
        hidden_grad = jnp.einsum(
            "rd,fd->rf", cot_rows, ffdown_back, preferred_element_type=jnp.float32
        )
        ffdown_w_grad = jnp.einsum(
            "rf,rd->fd", hidden_low, cot_rows, preferred_element_type=jnp.float32
        )
        gate_grad_low = (
            hidden_grad * up_ffn * gate_sigm * (1.0 + gate_ffn * (1.0 - gate_sigm))
        ).astype(jnp.bfloat16)
        up_grad_low = (hidden_grad * silu_gate).astype(jnp.bfloat16)
        ffgate_w_grad = jnp.einsum(
            "rd,rf->df", ffn_rows, gate_grad_low, preferred_element_type=jnp.float32
        )
        ffup_w_grad = jnp.einsum(
            "rd,rf->df", ffn_rows, up_grad_low, preferred_element_type=jnp.float32
        )
        ffn_in_part = jnp.einsum(
            "rf,df->rd", gate_grad_low, ffgate_back, preferred_element_type=jnp.float32
        ) + jnp.einsum("rf,df->rd", up_grad_low, ffup_back, preferred_element_type=jnp.float32)
        ffn_in_grad = lax.psum_scatter(
            ffn_in_part.reshape(seq_count, full_len, feature_dim).astype(jnp.bfloat16),
            "seq",
            scatter_dimension=1,
            tiled=True,
        ).astype(jnp.float32)
        middle_grad = cot_now.astype(jnp.float32) + rms_back(
            ffn_in_grad, normed_two, scale_two, ffn_gain
        )
        ffn_gain_sum = ffn_gain_sum + jnp.sum(ffn_in_grad * normed_two, axis=(0, 1))
        branch_rows = lax.all_gather(
            middle_grad.astype(jnp.bfloat16), "seq", axis=1, tiled=True
        ).reshape(row_count, feature_dim)
        gated_grad = jnp.einsum(
            "rd,ed->re", branch_rows, output_back, preferred_element_type=jnp.float32
        )
        output_w_grad = jnp.einsum(
            "re,rd->ed", gated_low, branch_rows, preferred_element_type=jnp.float32
        )
        attn_out_grad = (gated_grad * gate_sig).astype(jnp.bfloat16)
        outgate_pre_grad = (gated_grad * attn_out * gate_sig * (1.0 - gate_sig)).astype(
            jnp.bfloat16
        )
        back_items = (
            query_seq,
            key_seq,
            value_seq,
            attn_out_grad.reshape(seq_count, full_len, kv_heads, heads_per_group, HEAD_SIZE),
            log_totals,
            positions,
            doc_rows,
        )
        query_grad_raw, key_grad_raw, value_grad_raw = lax.map(
            partial(attend_backward, score_scale=score_scale), back_items
        )
        query_turned = rotate_back(
            query_grad_raw.reshape(row_count, query_heads, HEAD_SIZE), cosine_lookup, sine_lookup
        )
        query_pre_grad = (
            rms_back(query_turned, query_normed, query_scale, query_gain)
            .astype(jnp.bfloat16)
            .reshape(row_count, query_heads * HEAD_SIZE)
        )
        query_gain_sum = query_gain_sum + jnp.sum(query_turned * query_normed, axis=(0, 1))
        key_turned = rotate_back(
            key_grad_raw.reshape(row_count, kv_heads, HEAD_SIZE), cosine_lookup, sine_lookup
        )
        key_pre_grad = (
            rms_back(key_turned, key_normed, key_scale, key_gain)
            .astype(jnp.bfloat16)
            .reshape(row_count, kv_heads * HEAD_SIZE)
        )
        key_gain_sum = key_gain_sum + jnp.sum(key_turned * key_normed, axis=(0, 1))
        value_pre_grad = value_grad_raw.reshape(row_count, kv_heads * HEAD_SIZE).astype(
            jnp.bfloat16
        )
        query_w_grad = jnp.einsum(
            "rd,re->de", attn_rows, query_pre_grad, preferred_element_type=jnp.float32
        )
        key_w_grad = jnp.einsum(
            "rd,re->de", attn_rows, key_pre_grad, preferred_element_type=jnp.float32
        )
        value_w_grad = jnp.einsum(
            "rd,re->de", attn_rows, value_pre_grad, preferred_element_type=jnp.float32
        )
        outgate_w_grad = jnp.einsum(
            "rd,re->de", attn_rows, outgate_pre_grad, preferred_element_type=jnp.float32
        )
        attn_in_part = jnp.einsum(
            "re,de->rd", query_pre_grad, query_back, preferred_element_type=jnp.float32
        )
        attn_in_part = attn_in_part + jnp.einsum(
            "re,de->rd", key_pre_grad, key_back, preferred_element_type=jnp.float32
        )
        attn_in_part = attn_in_part + jnp.einsum(
            "re,de->rd", value_pre_grad, value_back, preferred_element_type=jnp.float32
        )
        attn_in_part = attn_in_part + jnp.einsum(
            "re,de->rd", outgate_pre_grad, outgate_back, preferred_element_type=jnp.float32
        )
        attn_in_grad = lax.psum_scatter(
            attn_in_part.reshape(seq_count, full_len, feature_dim).astype(jnp.bfloat16),
            "seq",
            scatter_dimension=1,
            tiled=True,
        ).astype(jnp.float32)
        input_now_grad = middle_grad + rms_back(
            attn_in_grad, first_normalized, scale_one, attn_gain
        )
        attn_gain_sum = attn_gain_sum + jnp.sum(attn_in_grad * first_normalized, axis=(0, 1))
        input_grads.append(input_now_grad.astype(jnp.bfloat16))
        scattered = (
            lax.psum_scatter(
                query_w_grad.astype(jnp.bfloat16), "fsdp", scatter_dimension=0, tiled=True
            ).astype(jnp.float32),
            lax.psum_scatter(
                key_w_grad.astype(jnp.bfloat16), "fsdp", scatter_dimension=0, tiled=True
            ).astype(jnp.float32),
            lax.psum_scatter(
                value_w_grad.astype(jnp.bfloat16), "fsdp", scatter_dimension=0, tiled=True
            ).astype(jnp.float32),
            lax.psum_scatter(
                outgate_w_grad.astype(jnp.bfloat16), "fsdp", scatter_dimension=0, tiled=True
            ).astype(jnp.float32),
            lax.psum_scatter(
                output_w_grad.astype(jnp.bfloat16), "fsdp", scatter_dimension=1, tiled=True
            ).astype(jnp.float32),
            lax.psum_scatter(
                ffgate_w_grad.astype(jnp.bfloat16), "fsdp", scatter_dimension=0, tiled=True
            ).astype(jnp.float32),
            lax.psum_scatter(
                ffup_w_grad.astype(jnp.bfloat16), "fsdp", scatter_dimension=0, tiled=True
            ).astype(jnp.float32),
            lax.psum_scatter(
                ffdown_w_grad.astype(jnp.bfloat16), "fsdp", scatter_dimension=1, tiled=True
            ).astype(jnp.float32),
        )
        grad_sums = tuple(
            (total_part + fresh_part for total_part, fresh_part in zip(grad_sums, scattered))
        )
    gain_totals = lax.psum(
        (attn_gain_sum, ffn_gain_sum, query_gain_sum, key_gain_sum), ("seq", "fsdp")
    )
    return (
        jnp.stack(outputs),
        jnp.stack(input_grads),
        grad_sums[0],
        grad_sums[1],
        grad_sums[2],
        grad_sums[3],
        grad_sums[4],
        grad_sums[5],
        grad_sums[6],
        grad_sums[7],
        gain_totals[0],
        gain_totals[1],
        gain_totals[2],
        gain_totals[3],
    )


def solution(mesh):
    return jax.shard_map(
        shards,
        mesh=mesh,
        in_specs=(
            P(None, "fsdp", "seq", None),
            P(None, "fsdp", "seq", None),
            P("fsdp", "seq"),
            P("fsdp", "seq"),
            P("fsdp", "seq"),
            P("fsdp", "seq"),
            P("seq", "fsdp"),
            P("fsdp", "seq"),
            P("fsdp", "seq"),
            P("seq", "fsdp"),
            P(),
            P(),
            P(),
            P(),
            P(None, "fsdp", None),
            P(None, "fsdp", None),
        ),
        out_specs=(
            P(None, "fsdp", "seq", None),
            P(None, "fsdp", "seq", None),
            P("fsdp", "seq"),
            P("fsdp", "seq"),
            P("fsdp", "seq"),
            P("fsdp", "seq"),
            P("seq", "fsdp"),
            P("fsdp", "seq"),
            P("fsdp", "seq"),
            P("seq", "fsdp"),
            P(),
            P(),
            P(),
            P(),
        ),
        check_vma=False,
    )
```

profile of v0, /device:TPU:0, one launch (start us, length us, event | category | flops | bytes accessed | tf_op | source)
XLA Modules:
  0.0 2203.6 jit_solution(11254966441913043898)
XLA Ops:
  36.9 28.1 %all-gather.25.cloned.1.call-done = bf16[2048,512]{1,0:T(8,128)(2,1)} async-done(((bf16[256,512]{1,0:T(8,128)(2,1)}), bf16[2048,512]{1,0:T(8,128)(2,1)}) %all-gather.25.cloned.1.call-update) | async-done | bytes 2097168 | tf_op jit(solution)/shard_map/all_gather | solution.py:189
  69.1 50.3 %all-gather.39.cloned.1.call-done = bf16[1,1024,2048]{2,1,0:T(8,128)(2,1)} async-done(((bf16[1,256,2048]{2,1,0:T(8,128)(2,1)}), bf16[1,1024,2048]{2,1,0:T(8,128)(2,1)}) %all-gather.39.cloned.1.call-update) | async-done | bytes 4194320 | tf_op jit(solution)/shard_map/all_gather | solution.py:185
  123.3 51.0 %all-gather.19.cloned.1.call-done = bf16[1,1024,2048]{2,1,0:T(8,128)(2,1)} async-done(((bf16[1,256,2048]{2,1,0:T(8,128)(2,1)}), bf16[1,1024,2048]{2,1,0:T(8,128)(2,1)}) %all-gather.19.cloned.1.call-update) | async-done | bytes 4194320 | tf_op jit(solution)/shard_map/all_gather | solution.py:185
  216.0 12.2 all-gather.27.cloned.1.call-done
  235.7 24.2 %all-gather.29.cloned.1.call-done = bf16[512,2048]{1,0:T(8,128)(2,1)} async-done(((bf16[512,256]{1,0:T(8,128)(2,1)}), bf16[512,2048]{1,0:T(8,128)(2,1)}) %all-gather.29.cloned.1.call-update) | async-done | bytes 2097168 | tf_op jit(solution)/shard_map/all_gather | solution.py:193
  296.2 56.5 %reduce-scatter.25.cloned.1.call-done = f32[1,256,2048]{2,1,0:T(8,128)} async-done(((f32[1,1024,2048]{2,1,0:T(8,128)}), f32[1,256,2048]{2,1,0:T(8,128)}) %reduce-scatter.25.cloned.1.call-update) | async-done | bytes 2097168 | tf_op jit(solution)/shard_map/reduce_scatter | solution.py:231
  352.7 89.4 %reduce-scatter.29.cloned.1.call-done = f32[1,256,2048]{2,1,0:T(8,128)} async-done(((f32[1,1024,2048]{2,1,0:T(8,128)}), f32[1,256,2048]{2,1,0:T(8,128)}) %reduce-scatter.29.cloned.1.call-update) | async-done | bytes 2097168 | tf_op jit(solution)/shard_map/reduce_scatter | solution.py:231
  451.5 56.9 %all-gather.35.cloned.1.call-done = bf16[2048,1536]{1,0:T(8,128)(2,1)} async-done(((bf16[256,1536]{1,0:T(8,128)(2,1)}), bf16[2048,1536]{1,0:T(8,128)(2,1)}) %all-gather.35.cloned.1.call-update) | async-done | bytes 6291472 | tf_op jit(solution)/shard_map/all_gather | solution.py:239
  508.4 53.7 %all-gather.31.cloned.1.call-done = bf16[1,1024,2048]{2,1,0:T(8,128)(2,1)} async-done(((bf16[1,256,2048]{2,1,0:T(8,128)(2,1)}), bf16[1,1024,2048]{2,1,0:T(8,128)(2,1)}) %all-gather.31.cloned.1.call-update) | async-done | bytes 4194320 | tf_op jit(solution)/shard_map/all_gather | solution.py:234
  562.0 11.9 fusion.74
  574.0 54.3 %all-gather.33.cloned.1.call-done = bf16[2048,1536]{1,0:T(8,128)(2,1)} async-done(((bf16[256,1536]{1,0:T(8,128)(2,1)}), bf16[2048,1536]{1,0:T(8,128)(2,1)}) %all-gather.33.cloned.1.call-update) | async-done | bytes 6291472 | tf_op jit(solution)/shard_map/all_gather | solution.py:238
  628.3 11.8 fusion.76
  640.0 41.9 %all-gather.47.cloned.1.call-done = bf16[1,1,1024,2048]{3,2,1,0:T(8,128)(2,1)} async-done(((bf16[1,1,256,2048]{3,2,1,0:T(8,128)(2,1)}), bf16[1,1,1024,2048]{3,2,1,0:T(8,128)(2,1)}) %all-gather.47.cloned.1.call-update) | async-done | bytes 4194320 | tf_op jit(solution)/shard_map/all_gather | solution.py:272
  681.9 66.6 %all-gather.37.cloned.1.call-done = bf16[1536,2048]{1,0:T(8,128)(2,1)} async-done(((bf16[1536,256]{1,0:T(8,128)(2,1)}), bf16[1536,2048]{1,0:T(8,128)(2,1)}) %all-gather.37.cloned.1.call-update) | async-done | bytes 6291472 | tf_op jit(solution)/shard_map/all_gather | solution.py:240
  748.6 17.0 multiply_convert_fusion.2
  783.6 50.9 %reduce-scatter.33.cloned.1.call-done = bf16[1,256,2048]{2,1,0:T(8,128)(2,1)} async-done(((bf16[1,1024,2048]{2,1,0:T(8,128)(2,1)}), bf16[1,256,2048]{2,1,0:T(8,128)(2,1)}) %reduce-scatter.33.cloned.1.call-update) | async-done | bytes 1048592 | tf_op jit(solution)/shard_map/reduce_scatter | solution.py:294
  839.5 52.1 %all-gather.41.cloned.1.call-done = bf16[1,1024,2048]{2,1,0:T(8,128)(2,1)} async-done(((bf16[1,256,2048]{2,1,0:T(8,128)(2,1)}), bf16[1,1024,2048]{2,1,0:T(8,128)(2,1)}) %all-gather.41.cloned.1.call-update) | async-done | bytes 4194320 | tf_op jit(solution)/shard_map/all_gather | solution.py:234
  891.6 12.5 fusion.52
  914.6 31.9 %all-gather.49.cloned.1.call-done = bf16[1,1,1024,2048]{3,2,1,0:T(8,128)(2,1)} async-done(((bf16[1,1,256,2048]{3,2,1,0:T(8,128)(2,1)}), bf16[1,1,1024,2048]{3,2,1,0:T(8,128)(2,1)}) %all-gather.49.cloned.1.call-update) | async-done | bytes 4194320 | tf_op jit(solution)/shard_map/all_gather | solution.py:272
  946.5 15.9 multiply_convert_fusion
  996.2 41.5 %reduce-scatter.37.cloned.1.call-done = bf16[1,256,2048]{2,1,0:T(8,128)(2,1)} async-done(((bf16[1,1024,2048]{2,1,0:T(8,128)(2,1)}), bf16[1,256,2048]{2,1,0:T(8,128)(2,1)}) %reduce-scatter.37.cloned.1.call-update) | async-done | bytes 1048592 | tf_op jit(solution)/shard_map/reduce_scatter | solution.py:294
  1040.3 53.0 %reduce-scatter.31.cloned.1.call-done = bf16[1,256,2048]{2,1,0:T(8,128)(2,1)} async-done(((bf16[1,1024,2048]{2,1,0:T(8,128)(2,1)}), bf16[1,256,2048]{2,1,0:T(8,128)(2,1)}) %reduce-scatter.31.cloned.1.call-update) | async-done | bytes 1048592 | tf_op jit(solution)/shard_map/reduce_scatter | solution.py:248
  1098.7 11.4 convolution_convert_fusion.1
  1125.2 11.7 convolution_convert_fusion.5
  1189.7 14.0 fusion.203
  1218.0 15.2 broadcast_multiply_fusion.1
  1274.9 14.4 fusion.200
  1289.3 17.7 broadcast_multiply_fusion
  1337.7 16.3 fusion.208
  1361.0 16.1 fusion.209
  1378.8 16.7 fusion.206
  1395.4 16.4 fusion.207
  1498.4 61.1 %reduce-scatter.65.cloned.1.call-done = bf16[256,1536]{1,0:T(8,128)(2,1)} async-done(((bf16[2048,1536]{1,0:T(8,128)(2,1)}), bf16[256,1536]{1,0:T(8,128)(2,1)}) %reduce-scatter.65.cloned.1.call-update) | async-done | bytes 786448 | tf_op jit(solution)/shard_map/reduce_scatter | solution.py:404
  1559.6 70.4 %reduce-scatter.67.cloned.1.call-done = bf16[256,1536]{1,0:T(8,128)(2,1)} async-done(((bf16[2048,1536]{1,0:T(8,128)(2,1)}), bf16[256,1536]{1,0:T(8,128)(2,1)}) %reduce-scatter.67.cloned.1.call-update) | async-done | bytes 786448 | tf_op jit(solution)/shard_map/reduce_scatter | solution.py:404
  1632.7 30.6 %reduce-scatter.51.cloned.1.call-done = bf16[256,256]{1,0:T(8,128)(2,1)} async-done(((bf16[2048,256]{1,0:T(8,128)(2,1)}), bf16[256,256]{1,0:T(8,128)(2,1)}) %reduce-scatter.51.cloned.1.call-update) | async-done | bytes 131088 | tf_op jit(solution)/shard_map/reduce_scatter | solution.py:392
  1663.3 33.1 %reduce-scatter.49.cloned.1.call-done = bf16[256,256]{1,0:T(8,128)(2,1)} async-done(((bf16[2048,256]{1,0:T(8,128)(2,1)}), bf16[256,256]{1,0:T(8,128)(2,1)}) %reduce-scatter.49.cloned.1.call-update) | async-done | bytes 131088 | tf_op jit(solution)/shard_map/reduce_scatter | solution.py:392
  1698.1 31.3 %reduce-scatter.47.cloned.1.call-done = bf16[256,256]{1,0:T(8,128)(2,1)} async-done(((bf16[2048,256]{1,0:T(8,128)(2,1)}), bf16[256,256]{1,0:T(8,128)(2,1)}) %reduce-scatter.47.cloned.1.call-update) | async-done | bytes 131088 | tf_op jit(solution)/shard_map/reduce_scatter | solution.py:389
  1729.4 33.1 %reduce-scatter.45.cloned.1.call-done = bf16[256,256]{1,0:T(8,128)(2,1)} async-done(((bf16[2048,256]{1,0:T(8,128)(2,1)}), bf16[256,256]{1,0:T(8,128)(2,1)}) %reduce-scatter.45.cloned.1.call-update) | async-done | bytes 131088 | tf_op jit(solution)/shard_map/reduce_scatter | solution.py:389
  1764.2 34.7 %reduce-scatter.57.cloned.1.call-done = bf16[512,256]{1,0:T(8,128)(2,1)} async-done(((bf16[512,2048]{1,0:T(8,128)(2,1)}), bf16[512,256]{1,0:T(8,128)(2,1)}) %reduce-scatter.57.cloned.1.call-update) | async-done | bytes 262160 | tf_op jit(solution)/shard_map/reduce_scatter | solution.py:398
  1798.9 37.0 %reduce-scatter.59.cloned.1.call-done = bf16[512,256]{1,0:T(8,128)(2,1)} async-done(((bf16[512,2048]{1,0:T(8,128)(2,1)}), bf16[512,256]{1,0:T(8,128)(2,1)}) %reduce-scatter.59.cloned.1.call-update) | async-done | bytes 262160 | tf_op jit(solution)/shard_map/reduce_scatter | solution.py:398
  1837.8 35.1 %reduce-scatter.55.cloned.1.call-done = bf16[256,512]{1,0:T(8,128)(2,1)} async-done(((bf16[2048,512]{1,0:T(8,128)(2,1)}), bf16[256,512]{1,0:T(8,128)(2,1)}) %reduce-scatter.55.cloned.1.call-update) | async-done | bytes 262160 | tf_op jit(solution)/shard_map/reduce_scatter | solution.py:395
  1872.9 37.0 %reduce-scatter.53.cloned.1.call-done = bf16[256,512]{1,0:T(8,128)(2,1)} async-done(((bf16[2048,512]{1,0:T(8,128)(2,1)}), bf16[256,512]{1,0:T(8,128)(2,1)}) %reduce-scatter.53.cloned.1.call-update) | async-done | bytes 262160 | tf_op jit(solution)/shard_map/reduce_scatter | solution.py:395
  1911.8 35.5 %reduce-scatter.41.cloned.1.call-done = bf16[256,512]{1,0:T(8,128)(2,1)} async-done(((bf16[2048,512]{1,0:T(8,128)(2,1)}), bf16[256,512]{1,0:T(8,128)(2,1)}) %reduce-scatter.41.cloned.1.call-update) | async-done | bytes 262160 | tf_op jit(solution)/shard_map/reduce_scatter | solution.py:386
  1947.3 37.4 %reduce-scatter.43.cloned.1.call-done = bf16[256,512]{1,0:T(8,128)(2,1)} async-done(((bf16[2048,512]{1,0:T(8,128)(2,1)}), bf16[256,512]{1,0:T(8,128)(2,1)}) %reduce-scatter.43.cloned.1.call-update) | async-done | bytes 262160 | tf_op jit(solution)/shard_map/reduce_scatter | solution.py:386
  1986.7 52.4 %reduce-scatter.35.cloned.1.call-done = bf16[1,256,2048]{2,1,0:T(8,128)(2,1)} async-done(((bf16[1,1024,2048]{2,1,0:T(8,128)(2,1)}), bf16[1,256,2048]{2,1,0:T(8,128)(2,1)}) %reduce-scatter.35.cloned.1.call-update) | async-done | bytes 1048592 | tf_op jit(solution)/shard_map/reduce_scatter | solution.py:374
  2039.0 55.5 %reduce-scatter.39.cloned.1.call-done = bf16[1,256,2048]{2,1,0:T(8,128)(2,1)} async-done(((bf16[1,1024,2048]{2,1,0:T(8,128)(2,1)}), bf16[1,256,2048]{2,1,0:T(8,128)(2,1)}) %reduce-scatter.39.cloned.1.call-update) | async-done | bytes 1048592 | tf_op jit(solution)/shard_map/reduce_scatter | solution.py:374
  2101.5 48.6 %reduce-scatter.27.cloned.1.call-done = bf16[1,256,2048]{2,1,0:T(8,128)(2,1)} async-done(((bf16[1,1024,2048]{2,1,0:T(8,128)(2,1)}), bf16[1,256,2048]{2,1,0:T(8,128)(2,1)}) %reduce-scatter.27.cloned.1.call-update) | async-done | bytes 1048592 | tf_op jit(solution)/shard_map/reduce_scatter | solution.py:248
  2156.6 39.7 %all-reduce = (f32[2048]{0:T(1024)}, f32[2048]{0:T(1024)}, f32[128]{0:T(128)}, f32[128]{0:T(128)}) all-reduce(f32[2048]{0:T(1024)S(1)} %add.500, f32[2048]{0:T(1024)S(1)} %add.501, f32[128]{0:T(128)S(1)} %add.502, f32[128]{0:T(128)S(1)} %add.503), channel_id=1, replica_groups=mesh['seq'=4,'fsdp'=8] {'seq','fsdp'}, use_global_device_ids=true, to_apply=%region_54.56 | all-reduce | flops 4352 | bytes 34816 | tf_op jit(solution)/shard_map/psum | solution.py:414
  (555 shorter events, 480.5 us)
Async XLA Ops:
  7.2 27.5 %all-gather.23.cloned.1.call-start = ((), (), s32[]{:S(2)}) async-start(), calls=%async_computation.26 | async-start | bytes 1179648 | tf_op jit(solution)/shard_map/all_gather | solution.py:190
  7.9 57.1 %all-gather.25.cloned.1.call-start = ((), (), s32[]{:S(2)}) async-start(), calls=%async_computation.27 | async-start | bytes 2359296 | tf_op jit(solution)/shard_map/all_gather | solution.py:189
  8.7 110.8 %all-gather.39.cloned.1.call-start = ((), (), s32[]{:S(2)}) async-start(), calls=%async_computation.36 | async-start | bytes 5242880 | tf_op jit(solution)/shard_map/all_gather | solution.py:185
  14.8 159.5 %all-gather.19.cloned.1.call-start = ((), (), s32[]{:S(2)}) async-start(), calls=%async_computation.24 | async-start | bytes 5242880 | tf_op jit(solution)/shard_map/all_gather | solution.py:185
  15.4 188.0 %all-gather.21.cloned.1.call-start = ((), (), s32[]{:S(2)}) async-start(), calls=%async_computation.25 | async-start | bytes 1179648 | tf_op jit(solution)/shard_map/all_gather | solution.py:191
  16.0 212.3 %all-gather.27.cloned.1.call-start = ((), (), s32[]{:S(2)}) async-start(), calls=%async_computation.28 | async-start | bytes 2359296 | tf_op jit(solution)/shard_map/all_gather | solution.py:192
  16.5 243.4 %all-gather.29.cloned.1.call-start = ((), (), s32[]{:S(2)}) async-start(), calls=%async_computation.29 | async-start | bytes 2359296 | tf_op jit(solution)/shard_map/all_gather | solution.py:193
  17.3 335.4 %reduce-scatter.25.cloned.1.call-start = ((), (), s32[]{:S(2)}) async-start(), calls=%async_computation.30 | async-start | bytes 10485760 | tf_op jit(solution)/shard_map/reduce_scatter | solution.py:231
  267.3 174.9 %reduce-scatter.29.cloned.1.call-start = ((), (), s32[]{:S(2)}) async-start(), calls=%async_computation.37 | async-start | bytes 10485760 | tf_op jit(solution)/shard_map/reduce_scatter | solution.py:231
  295.6 212.8 %all-gather.35.cloned.1.call-start = ((), (), s32[]{:S(2)}) async-start(), calls=%async_computation.33 | async-start | bytes 7077888 | tf_op jit(solution)/shard_map/all_gather | solution.py:239
  296.2 265.9 %all-gather.31.cloned.1.call-start = ((), (), s32[]{:S(2)}) async-start(), calls=%async_computation.31 | async-start | bytes 5242880 | tf_op jit(solution)/shard_map/all_gather | solution.py:234
  446.2 647.0 %copy-start.102 = (f32[256]{0:T(256)}, f32[256]{0:T(256)S(1)}, u32[]{:S(2)}) copy-start(f32[256]{0:T(256)S(1)} %add_rsqrt_fusion.6) | copy-start | bytes 3076
  448.7 179.5 %all-gather.33.cloned.1.call-start = ((), (), s32[]{:S(2)}) async-start(), calls=%async_computation.32 | async-start | bytes 7077888 | tf_op jit(solution)/shard_map/all_gather | solution.py:238
  449.3 232.6 %all-gather.47.cloned.1.call-start = ((), (), s32[]{:S(2)}) async-start(), calls=%async_computation.62 | async-start | bytes 5242880 | tf_op jit(solution)/shard_map/all_gather | solution.py:272
  450.9 297.7 %all-gather.37.cloned.1.call-start = ((), (), s32[]{:S(2)}) async-start(), calls=%async_computation.34 | async-start | bytes 7077888 | tf_op jit(solution)/shard_map/all_gather | solution.py:240
  451.4 383.0 %reduce-scatter.33.cloned.1.call-start = ((), (), s32[]{:S(2)}) async-start(), calls=%async_computation.40 | async-start | bytes 5242880 | tf_op jit(solution)/shard_map/reduce_scatter | solution.py:294
  783.5 108.1 %all-gather.41.cloned.1.call-start = ((), (), s32[]{:S(2)}) async-start(), calls=%async_computation.38 | async-start | bytes 5242880 | tf_op jit(solution)/shard_map/all_gather | solution.py:234
  838.9 107.6 %all-gather.49.cloned.1.call-start = ((), (), s32[]{:S(2)}) async-start(), calls=%async_computation.63 | async-start | bytes 5242880 | tf_op jit(solution)/shard_map/all_gather | solution.py:272
  839.5 198.2 %reduce-scatter.37.cloned.1.call-start = ((), (), s32[]{:S(2)}) async-start(), calls=%async_computation.43 | async-start | bytes 5242880 | tf_op jit(solution)/shard_map/reduce_scatter | solution.py:294
  984.9 108.3 %reduce-scatter.31.cloned.1.call-start = ((), (), s32[]{:S(2)}) async-start(), calls=%async_computation.39 | async-start | bytes 5242880 | tf_op jit(solution)/shard_map/reduce_scatter | solution.py:248
  996.1 180.4 %all-gather.43.cloned.1.call-start = ((), (), s32[]{:S(2)}) async-start(), calls=%async_computation.41 | async-start | bytes 5242880 | tf_op jit(solution)/shard_map/all_gather | solution.py:304
  1097.9 107.7 %all-gather.45.cloned.1.call-start = ((), (), s32[]{:S(2)}) async-start(), calls=%async_computation.44 | async-start | bytes 5242880 | tf_op jit(solution)/shard_map/all_gather | solution.py:304
  1098.7 394.1 %reduce-scatter.69.cloned.1.call-start = ((), (), s32[]{:S(2)}) async-start(), calls=%async_computation.60 | async-start | bytes 7077888 | tf_op jit(solution)/shard_map/reduce_scatter | solution.py:407
  1110.2 382.6 %reduce-scatter.71.cloned.1.call-start = ((), (), s32[]{:S(2)}) async-start(), calls=%async_computation.61 | async-start | bytes 7077888 | tf_op jit(solution)/shard_map/reduce_scatter | solution.py:407
  1123.3 372.1 %reduce-scatter.61.cloned.1.call-start = ((), (), s32[]{:S(2)}) async-start(), calls=%async_computation.56 | async-start | bytes 7077888 | tf_op jit(solution)/shard_map/reduce_scatter | solution.py:401
  1136.9 358.6 %reduce-scatter.63.cloned.1.call-start = ((), (), s32[]{:S(2)}) async-start(), calls=%async_computation.57 | async-start | bytes 7077888 | tf_op jit(solution)/shard_map/reduce_scatter | solution.py:401
  1149.8 409.8 %reduce-scatter.65.cloned.1.call-start = ((), (), s32[]{:S(2)}) async-start(), calls=%async_computation.58 | async-start | bytes 7077888 | tf_op jit(solution)/shard_map/reduce_scatter | solution.py:404
  1162.8 467.1 %reduce-scatter.67.cloned.1.call-start = ((), (), s32[]{:S(2)}) async-start(), calls=%async_computation.59 | async-start | bytes 7077888 | tf_op jit(solution)/shard_map/reduce_scatter | solution.py:404
  1175.8 487.5 %reduce-scatter.51.cloned.1.call-start = ((), (), s32[]{:S(2)}) async-start(), calls=%async_computation.51 | async-start | bytes 1179648 | tf_op jit(solution)/shard_map/reduce_scatter | solution.py:392
  1254.2 442.2 %reduce-scatter.49.cloned.1.call-start = ((), (), s32[]{:S(2)}) async-start(), calls=%async_computation.50 | async-start | bytes 1179648 | tf_op jit(solution)/shard_map/reduce_scatter | solution.py:392
  1274.9 454.5 %reduce-scatter.47.cloned.1.call-start = ((), (), s32[]{:S(2)}) async-start(), calls=%async_computation.49 | async-start | bytes 1179648 | tf_op jit(solution)/shard_map/reduce_scatter | solution.py:389
  1314.2 448.3 %reduce-scatter.45.cloned.1.call-start = ((), (), s32[]{:S(2)}) async-start(), calls=%async_computation.48 | async-start | bytes 1179648 | tf_op jit(solution)/shard_map/reduce_scatter | solution.py:389
  1318.9 480.0 %reduce-scatter.57.cloned.1.call-start = ((), (), s32[]{:S(2)}) async-start(), calls=%async_computation.54 | async-start | bytes 2359296 | tf_op jit(solution)/shard_map/reduce_scatter | solution.py:398
  1325.0 510.9 %reduce-scatter.59.cloned.1.call-start = ((), (), s32[]{:S(2)}) async-start(), calls=%async_computation.55 | async-start | bytes 2359296 | tf_op jit(solution)/shard_map/reduce_scatter | solution.py:398
  1331.6 541.4 %reduce-scatter.55.cloned.1.call-start = ((), (), s32[]{:S(2)}) async-start(), calls=%async_computation.53 | async-start | bytes 2359296 | tf_op jit(solution)/shard_map/reduce_scatter | solution.py:395
  1337.7 572.3 %reduce-scatter.53.cloned.1.call-start = ((), (), s32[]{:S(2)}) async-start(), calls=%async_computation.52 | async-start | bytes 2359296 | tf_op jit(solution)/shard_map/reduce_scatter | solution.py:395
  1360.5 586.8 %reduce-scatter.41.cloned.1.call-start = ((), (), s32[]{:S(2)}) async-start(), calls=%async_computation.46 | async-start | bytes 2359296 | tf_op jit(solution)/shard_map/reduce_scatter | solution.py:386
  1425.0 559.7 %reduce-scatter.43.cloned.1.call-start = ((), (), s32[]{:S(2)}) async-start(), calls=%async_computation.47 | async-start | bytes 2359296 | tf_op jit(solution)/shard_map/reduce_scatter | solution.py:386
  1432.5 606.6 %reduce-scatter.35.cloned.1.call-start = ((), (), s32[]{:S(2)}) async-start(), calls=%async_computation.42 | async-start | bytes 5242880 | tf_op jit(solution)/shard_map/reduce_scatter | solution.py:374
  1455.4 639.1 %reduce-scatter.39.cloned.1.call-start = ((), (), s32[]{:S(2)}) async-start(), calls=%async_computation.45 | async-start | bytes 5242880 | tf_op jit(solution)/shard_map/reduce_scatter | solution.py:374
  1479.2 670.9 %reduce-scatter.27.cloned.1.call-start = ((), (), s32[]{:S(2)}) async-start(), calls=%async_computation.35 | async-start | bytes 5242880 | tf_op jit(solution)/shard_map/reduce_scatter | solution.py:248
  1498.4 596.1 %copy-start.5 = (bf16[2,1,256,2048]{3,2,1,0:T(8,128)(2,1)S(1)}, bf16[2,1,256,2048]{3,2,1,0:T(8,128)(2,1)}, u32[]{:S(2)}) copy-start(bf16[2,1,256,2048]{3,2,1,0:T(8,128)(2,1)} %param.18) | copy-start | bytes 6291460
  1498.4 596.1 %copy-start.79 = (f32[2048]{0:T(1024)S(1)}, f32[2048]{0:T(1024)}, u32[]{:S(2)}) copy-start(f32[2048]{0:T(1024)} %param.28) | copy-start | bytes 24580
  1498.4 596.1 %copy-start.107 = (f32[256]{0:T(256)S(1)}, f32[256]{0:T(256)}, u32[]{:S(2)}) copy-start(f32[256]{0:T(256)} %copy-done.106) | copy-start | bytes 3076
  1498.4 596.1 %copy-start.109 = (f32[256]{0:T(256)S(1)}, f32[256]{0:T(256)}, u32[]{:S(2)}) copy-start(f32[256]{0:T(256)} %copy-done.108) | copy-start | bytes 3076
  1632.7 464.9 %copy-start.74 = (f32[2048]{0:T(1024)S(1)}, f32[2048]{0:T(1024)}, u32[]{:S(2)}) copy-start(f32[2048]{0:T(1024)} %param.29) | copy-start | bytes 24580
  1632.7 464.9 %copy-start.105 = (f32[256]{0:T(256)S(1)}, f32[256]{0:T(256)}, u32[]{:S(2)}) copy-start(f32[256]{0:T(256)} %copy-done.104) | copy-start | bytes 3076
  1632.7 464.9 %copy-start.113 = (f32[256]{0:T(256)S(1)}, f32[256]{0:T(256)}, u32[]{:S(2)}) copy-start(f32[256]{0:T(256)} %copy-done.112) | copy-start | bytes 3076
  (144 other events, 2565.6 us)
Sparse Core Ops, SparseCore 0:
  9.6 25.0 all-gather.22
  36.2 28.7 all-gather.24
  67.4 51.9 all-gather.38
  121.7 52.5 all-gather.18
  175.8 22.2 all-gather.20
  199.5 28.7 all-gather.26
  229.9 29.9 all-gather.28
  267.4 85.2 reduce-scatter.24
  355.8 86.3 reduce-scatter.28
  443.6 64.6 all-gather.34
  510.8 51.2 all-gather.30
  563.5 64.6 all-gather.32
  630.7 51.2 all-gather.46
  683.4 65.1 all-gather.36
  783.6 50.8 reduce-scatter.32
  839.0 52.5 all-gather.40
  893.9 52.5 all-gather.48
  985.0 52.5 reduce-scatter.36
  1040.6 52.5 reduce-scatter.30
  1098.1 52.5 all-gather.42
  1153.1 52.5 all-gather.44
  1208.0 69.7 reduce-scatter.68
  1280.0 68.1 reduce-scatter.70
  1350.5 68.1 reduce-scatter.60
  1421.0 68.1 reduce-scatter.62
  1491.3 68.1 reduce-scatter.64
  1561.7 68.1 reduce-scatter.66
  1632.2 31.0 reduce-scatter.50
  1665.6 30.7 reduce-scatter.48
  1698.5 30.7 reduce-scatter.46
  1731.6 30.7 reduce-scatter.44
  1764.8 34.0 reduce-scatter.56
  1801.0 34.8 reduce-scatter.58
  1838.2 34.6 reduce-scatter.54
  1875.2 34.6 reduce-scatter.52
  1912.6 34.6 reduce-scatter.40
  1950.0 34.6 reduce-scatter.42
  1987.7 51.2 reduce-scatter.34
  2041.8 52.5 reduce-scatter.38
  2097.5 52.5 reduce-scatter.26
where the time goes:
time: 2210 us; the launch traced here: 2200 us
  waiting for transfers between devices  1460 us (66%)
  matrix products  542 us (25%)
  other arithmetic  90 us (4%)
  local copies, waits for them, and re-layouts  51.5 us (2%)
  blocking collectives  39.7 us (2%)
    reduce_scatter x2, waiting for transfers between devices, shards(): lax.psum_scatter(attn_part, 'seq', scatter_dimension=1, tiled=True)  146 us
    reduce_scatter x2, waiting for transfers between devices, shards(): lax.psum_scatter(ffup_w_grad.astype(jnp.bfloat16), 'fsdp', scatter_dimens...  131 us
    dot_general x16, matrix products, dense(): return jnp.dot(left, right, preferred_element_type=jnp.float32)  114 us
    reduce_scatter x2, waiting for transfers between devices, shards(): lax.psum_scatter(attn_in_part.reshape(seq_count, full_len, feature_dim).a...  108 us
    all_gather x2, waiting for transfers between devices, shards(): lax.all_gather((normed_two * ffn_gain).astype(jnp.bfloat16), 'seq', axis=...  106 us
    reduce_scatter x2, waiting for transfers between devices, shards(): lax.psum_scatter(ffn_part.astype(jnp.bfloat16), 'seq', scatter_dimension=...  102 us
    all_gather x2, waiting for transfers between devices, shards(): lax.all_gather((first_normalized * attn_gain).astype(jnp.bfloat16), 'seq'...  101 us
    reduce_scatter x2, waiting for transfers between devices, shards(): lax.psum_scatter(ffn_in_part.reshape(seq_count, full_len, feature_dim).as...  92.4 us
  transfers between devices with their start and end apart: 40, of which 34 were waited for; matrix products, arithmetic and copies ran while one was open for 25% of the time, Pallas kernels for 0%

commit v1 on v0

v1 whole, which is shorter than its diff:
```python
import math

import jax
import jax.numpy as jnp
from jax import lax
from jax.sharding import PartitionSpec as P

HEAD_SIZE = 128


EPSILON = 1e-06
ROPE_BASE = 5000000.0
NEG_LARGE = -1e30


def rms_scale(values):
    return lax.rsqrt(jnp.mean(values * values, axis=-1, keepdims=True) + EPSILON)


def rms_back(grad_out, normed, scales, gain):
    scaled_grad = grad_out * gain
    return scales * (scaled_grad - normed * jnp.mean(scaled_grad * normed, axis=-1, keepdims=True))


def rope_tables(positions, head_dim):
    half_dim = head_dim // 2
    inverse = jnp.exp(
        -math.log(ROPE_BASE) * 2.0 * jnp.arange(half_dim, dtype=jnp.float32) / head_dim
    )
    angles = positions.astype(jnp.float32)[:, None] * inverse[None, :]
    cosines = jnp.cos(angles)
    sines = jnp.sin(angles)
    return (jnp.concatenate([cosines, cosines], -1), jnp.concatenate([sines, sines], -1))


def apply_rotary(values, cosine_lookup, sine_lookup):
    half_dim = values.shape[-1] // 2
    turned = jnp.concatenate([-values[..., half_dim:], values[..., :half_dim]], -1)
    return values * cosine_lookup + turned * sine_lookup


def rotate_back(values, cosine_lookup, sine_lookup):
    half_dim = values.shape[-1] // 2
    shifted = values * sine_lookup
    turned = jnp.concatenate([shifted[..., half_dim:], -shifted[..., :half_dim]], -1)
    return values * cosine_lookup + turned


def visible_mask(positions, doc_rows, begin_row, end_row):
    return (positions[None, :] <= positions[begin_row:end_row, None]) & (
        doc_rows[None, :] == doc_rows[begin_row:end_row, None]
    )


def block_scores(query_row_block, key_rows, positions, doc_rows, begin_row, end_row, score_scale):
    scores = (
        jnp.einsum(
            "qhgd,khd->hgqk",
            query_row_block[begin_row:end_row],
            key_rows,
            preferred_element_type=jnp.float32,
        )
        * score_scale
    )
    return jnp.where(visible_mask(positions, doc_rows, begin_row, end_row), scores, NEG_LARGE)


def attend_forward(item, score_scale):
    query_row_block, key_rows, value_row_block, positions, doc_rows = item
    sequence_length = query_row_block.shape[0]
    block_rows = min(512, sequence_length)
    outputs = []
    totals = []
    for begin_row in range(0, sequence_length, block_rows):
        end_row = begin_row + block_rows
        scores = block_scores(
            query_row_block, key_rows, positions, doc_rows, begin_row, end_row, score_scale
        )
        highest = jnp.max(scores, axis=-1, keepdims=True)
        exponents = jnp.exp(scores - highest)
        denominator = jnp.sum(exponents, axis=-1, keepdims=True)
        prob_low = (exponents / denominator).astype(jnp.bfloat16)
        outputs.append(
            jnp.einsum(
                "hgqk,khd->qhgd", prob_low, value_row_block, preferred_element_type=jnp.float32
            )
        )
        totals.append((highest + jnp.log(denominator))[..., 0])
    return (jnp.concatenate(outputs, 0), jnp.concatenate(totals, -1))


def attend_backward(item, score_scale):
    query_row_block, key_rows, value_row_block, out_grads, log_totals, positions, doc_rows = item
    sequence_length = query_row_block.shape[0]
    block_rows = min(512, sequence_length)
    key_sum = jnp.zeros(key_rows.shape, jnp.float32)
    value_sum = jnp.zeros(value_row_block.shape, jnp.float32)
    query_parts = []
    for begin_row in range(0, sequence_length, block_rows):
        end_row = begin_row + block_rows
        scores = block_scores(
            query_row_block, key_rows, positions, doc_rows, begin_row, end_row, score_scale
        )
        probs = jnp.exp(scores - log_totals[..., begin_row:end_row, None])
        prob_grad = jnp.einsum(
            "qhgd,khd->hgqk",
            out_grads[begin_row:end_row],
            value_row_block,
            preferred_element_type=jnp.float32,
        )
        score_grad = (
            probs * (prob_grad - jnp.sum(prob_grad * probs, axis=-1, keepdims=True)) * score_scale
        ).astype(jnp.bfloat16)
        query_parts.append(
            jnp.einsum("hgqk,khd->qhgd", score_grad, key_rows, preferred_element_type=jnp.float32)
        )
        key_sum = key_sum + jnp.einsum(
            "hgqk,qhgd->khd",
            score_grad,
            query_row_block[begin_row:end_row],
            preferred_element_type=jnp.float32,
        )
        value_sum = value_sum + jnp.einsum(
            "hgqk,qhgd->khd",
            probs.astype(jnp.bfloat16),
            out_grads[begin_row:end_row],
            preferred_element_type=jnp.float32,
        )
    return (jnp.concatenate(query_parts, 0), key_sum, value_sum)


def dense(left, right):
    return jnp.dot(left, right, preferred_element_type=jnp.float32)


def flips(count, bit):
    return [(index, index ^ bit) for index in range(count)]


def gather_tokens(own):
    count = lax.axis_size("seq")
    if count != 4:
        return lax.all_gather(own, "seq", axis=0, tiled=True)
    half = own.shape[0] // 2
    across = lax.ppermute(own, "seq", flips(4, 1))
    along = lax.ppermute(own, "seq", flips(4, 2))
    far_top = lax.ppermute(along[:half], "seq", flips(4, 1))
    far_bottom = lax.ppermute(across[half:], "seq", flips(4, 2))
    return jnp.concatenate([own, across, along, far_top, far_bottom], 0)


def scatter_tokens(part):
    count = lax.axis_size("seq")
    if count != 4:
        return lax.psum_scatter(
            part.astype(jnp.bfloat16), "seq", scatter_dimension=0, tiled=True
        ).astype(jnp.float32)
    rows = part.shape[0] // 8
    low = part.astype(jnp.bfloat16)
    own_top, own_bottom, across_top, across_bottom, along_top, along_bottom, far_top, far_bottom = (
        low[index * rows : (index + 1) * rows] for index in range(8)
    )

    def plus(left, right):
        return (left.astype(jnp.float32) + right.astype(jnp.float32)).astype(jnp.bfloat16)

    relay_top = lax.ppermute(far_top, "seq", flips(4, 1))
    relay_bottom = lax.ppermute(far_bottom, "seq", flips(4, 2))
    from_across_top = lax.ppermute(across_top, "seq", flips(4, 1))
    from_along_bottom = lax.ppermute(along_bottom, "seq", flips(4, 2))
    from_along_top = lax.ppermute(plus(along_top, relay_top), "seq", flips(4, 2))
    from_across_bottom = lax.ppermute(plus(across_bottom, relay_bottom), "seq", flips(4, 1))
    top = (
        own_top.astype(jnp.float32)
        + from_across_top.astype(jnp.float32)
        + from_along_top.astype(jnp.float32)
    )
    bottom = (
        own_bottom.astype(jnp.float32)
        + from_along_bottom.astype(jnp.float32)
        + from_across_bottom.astype(jnp.float32)
    )
    return jnp.concatenate([top, bottom], 0)


def sum_everywhere(value):
    for axis in ("seq", "fsdp"):
        count = lax.axis_size(axis)
        if count & (count - 1):
            value = lax.psum(value, axis)
            continue
        terms = [value] + [
            lax.ppermute(value, axis, flips(count, bit)) for bit in range(1, count)
        ]
        while len(terms) > 1:
            terms = [terms[at] + terms[at + 1] for at in range(0, len(terms), 2)]
        value = terms[0]
    return value


def gather_weight(shard):
    return lax.all_gather(shard, "fsdp", axis=0, tiled=True)


def scatter_weight(total):
    return lax.psum_scatter(
        total.astype(jnp.bfloat16), "fsdp", scatter_dimension=0, tiled=True
    ).astype(jnp.float32)


def times_transposed(left, right):
    return jnp.einsum("re,de->rd", left, right, preferred_element_type=jnp.float32)


def outer(left, right):
    return jnp.einsum("rd,rf->df", left, right, preferred_element_type=jnp.float32)


def shards(
    block_input,
    out_grad,
    query_proj,
    key_projection,
    value_projection,
    outgate_proj,
    output_proj,
    ffgate_proj,
    ffup_proj,
    ffdown_proj,
    attn_gain,
    ffn_gain,
    query_gain,
    key_gain,
    piece_order,
    doc_ids,
):
    seq_devices = lax.axis_size("seq")
    micro_count, seq_count, local_len, feature_dim = block_input.shape
    full_len = local_len * seq_devices
    piece_len = full_len // piece_order.shape[2]
    query_width = query_proj.shape[1]
    key_width = key_projection.shape[1]
    hidden_width = ffgate_proj.shape[1]
    query_heads = query_width // HEAD_SIZE
    kv_heads = key_width // HEAD_SIZE
    heads_per_group = query_heads // kv_heads
    score_scale = HEAD_SIZE ** (-0.5)
    cuts = [query_width, query_width + key_width, query_width + 2 * key_width]
    micros = range(micro_count)
    place = lax.axis_index("seq")
    owners = place ^ jnp.arange(seq_devices) if seq_devices == 4 else jnp.arange(seq_devices)

    inputs = [block_input[m, 0].astype(jnp.float32) for m in micros]
    scale_one = [rms_scale(x) for x in inputs]
    first_normalized = [x * s for x, s in zip(inputs, scale_one)]
    attn_rows = [gather_tokens((x * attn_gain).astype(jnp.bfloat16)) for x in first_normalized]
    qkvg_full = gather_weight(
        jnp.concatenate([query_proj, key_projection, value_projection, outgate_proj], 1)
    )
    output_full = gather_weight(output_proj.T)
    gate_up_full = gather_weight(jnp.concatenate([ffgate_proj, ffup_proj], 1))
    down_full = gather_weight(ffdown_proj.T)
    cot_rows = [gather_tokens(out_grad[m, 0]) for m in micros]

    kept = []
    middle, scale_two, normed_two, ffn_rows = [], [], [], []
    for m in micros:
        pre = dense(attn_rows[m], qkvg_full)
        query_pre, key_pre, value_pre, gate_pre = jnp.split(pre, cuts, axis=1)
        query_pre = query_pre.reshape(full_len, query_heads, HEAD_SIZE)
        key_pre = key_pre.reshape(full_len, kv_heads, HEAD_SIZE)
        value_low = value_pre.astype(jnp.bfloat16).reshape(full_len, kv_heads, HEAD_SIZE)
        stored = (
            piece_order[m, 0][:, None] * piece_len
            + jnp.arange(piece_len, dtype=jnp.int32)[None, :]
        ).reshape(seq_devices, local_len)
        positions = stored[owners].reshape(full_len)
        doc_rows = doc_ids[m, 0][positions]
        cosine_lookup, sine_lookup = rope_tables(positions, HEAD_SIZE)
        cosine_lookup = cosine_lookup[:, None, :]
        sine_lookup = sine_lookup[:, None, :]
        query_scale = rms_scale(query_pre)
        query_normed = query_pre * query_scale
        query_low = apply_rotary(query_normed * query_gain, cosine_lookup, sine_lookup).astype(
            jnp.bfloat16
        )
        key_scale = rms_scale(key_pre)
        key_normed = key_pre * key_scale
        key_low = apply_rotary(key_normed * key_gain, cosine_lookup, sine_lookup).astype(
            jnp.bfloat16
        )
        query_seq = query_low.reshape(full_len, kv_heads, heads_per_group, HEAD_SIZE)
        attn_out, log_totals = attend_forward(
            (query_seq, key_low, value_low, positions, doc_rows), score_scale
        )
        attn_out = attn_out.reshape(full_len, query_width)
        gate_sig = jax.nn.sigmoid(gate_pre)
        gated_low = (attn_out * gate_sig).astype(jnp.bfloat16)
        now = inputs[m] + scatter_tokens(times_transposed(gated_low, output_full))
        middle.append(now)
        scale_two.append(rms_scale(now))
        normed_two.append(now * scale_two[m])
        ffn_rows.append(gather_tokens((normed_two[m] * ffn_gain).astype(jnp.bfloat16)))
        kept.append(
            (
                query_seq,
                key_low,
                value_low,
                positions,
                doc_rows,
                cosine_lookup,
                sine_lookup,
                query_scale,
                query_normed,
                key_scale,
                key_normed,
                attn_out,
                log_totals,
                gate_sig,
                gated_low,
            )
        )

    hidden, gate_ffn, up_ffn = [], [], []
    for m in micros:
        gate_up = dense(ffn_rows[m], gate_up_full)
        gate_ffn.append(gate_up[:, :hidden_width])
        up_ffn.append(gate_up[:, hidden_width:])
        hidden.append((jax.nn.silu(gate_ffn[m]) * up_ffn[m]).astype(jnp.bfloat16))
    down_grad = scatter_weight(sum(outer(cot_rows[m], hidden[m]) for m in micros))
    outputs, gate_grad, up_grad, ffn_in_grad = [], [], [], []
    for m in micros:
        hidden_grad = dense(cot_rows[m], down_full)
        gate_sigm = jax.nn.sigmoid(gate_ffn[m])
        gate_grad.append(
            (
                hidden_grad * up_ffn[m] * gate_sigm * (1.0 + gate_ffn[m] * (1.0 - gate_sigm))
            ).astype(jnp.bfloat16)
        )
        up_grad.append((hidden_grad * (gate_ffn[m] * gate_sigm)).astype(jnp.bfloat16))
        part = times_transposed(gate_grad[m], gate_up_full[:, :hidden_width]) + times_transposed(
            up_grad[m], gate_up_full[:, hidden_width:]
        )
        ffn_in_grad.append(scatter_tokens(part))
    gate_w_grad = scatter_weight(sum(outer(ffn_rows[m], gate_grad[m]) for m in micros))
    up_w_grad = scatter_weight(sum(outer(ffn_rows[m], up_grad[m]) for m in micros))
    for m in micros:
        block_out = middle[m] + scatter_tokens(times_transposed(hidden[m], down_full))
        outputs.append(block_out.astype(jnp.bfloat16))

    middle_grad, branch_rows, ffn_gain_sum = [], [], 0.0
    for m in micros:
        middle_grad.append(
            out_grad[m, 0].astype(jnp.float32)
            + rms_back(ffn_in_grad[m], normed_two[m], scale_two[m], ffn_gain)
        )
        ffn_gain_sum = ffn_gain_sum + jnp.sum(ffn_in_grad[m] * normed_two[m], axis=0)
        branch_rows.append(gather_tokens(middle_grad[m].astype(jnp.bfloat16)))
    output_grad = scatter_weight(sum(outer(branch_rows[m], kept[m][-1]) for m in micros))

    query_gain_sum, key_gain_sum, attn_gain_sum = 0.0, 0.0, 0.0
    qkvg_sum = 0.0
    input_grads = []
    for m in micros:
        (
            query_seq,
            key_low,
            value_low,
            positions,
            doc_rows,
            cosine_lookup,
            sine_lookup,
            query_scale,
            query_normed,
            key_scale,
            key_normed,
            attn_out,
            log_totals,
            gate_sig,
            gated_low,
        ) = kept[m]
        gated_grad = dense(branch_rows[m], output_full)
        attn_out_grad = (gated_grad * gate_sig).astype(jnp.bfloat16)
        outgate_pre_grad = (gated_grad * attn_out * gate_sig * (1.0 - gate_sig)).astype(
            jnp.bfloat16
        )
        query_grad_raw, key_grad_raw, value_grad_raw = attend_backward(
            (
                query_seq,
                key_low,
                value_low,
                attn_out_grad.reshape(full_len, kv_heads, heads_per_group, HEAD_SIZE),
                log_totals,
                positions,
                doc_rows,
            ),
            score_scale,
        )
        query_turned = rotate_back(
            query_grad_raw.reshape(full_len, query_heads, HEAD_SIZE), cosine_lookup, sine_lookup
        )
        query_pre_grad = (
            rms_back(query_turned, query_normed, query_scale, query_gain)
            .astype(jnp.bfloat16)
            .reshape(full_len, query_width)
        )
        query_gain_sum = query_gain_sum + jnp.sum(query_turned * query_normed, axis=(0, 1))
        key_turned = rotate_back(key_grad_raw, cosine_lookup, sine_lookup)
        key_pre_grad = (
            rms_back(key_turned, key_normed, key_scale, key_gain)
            .astype(jnp.bfloat16)
            .reshape(full_len, key_width)
        )
        key_gain_sum = key_gain_sum + jnp.sum(key_turned * key_normed, axis=(0, 1))
        value_pre_grad = value_grad_raw.reshape(full_len, key_width).astype(jnp.bfloat16)
        pre_grad = jnp.concatenate(
            [query_pre_grad, key_pre_grad, value_pre_grad, outgate_pre_grad], 1
        )
        attn_in_grad = scatter_tokens(times_transposed(pre_grad, qkvg_full))
        qkvg_sum = qkvg_sum + outer(attn_rows[m], pre_grad)
        input_grads.append(
            (
                middle_grad[m]
                + rms_back(attn_in_grad, first_normalized[m], scale_one[m], attn_gain)
            ).astype(jnp.bfloat16)
        )
        attn_gain_sum = attn_gain_sum + jnp.sum(attn_in_grad * first_normalized[m], axis=0)
    query_w_grad, key_w_grad, value_w_grad, outgate_w_grad = jnp.split(
        scatter_weight(qkvg_sum), cuts, axis=1
    )
    gains = sum_everywhere(
        jnp.concatenate([attn_gain_sum, ffn_gain_sum, query_gain_sum, key_gain_sum])
    )
    return (
        jnp.stack(outputs)[:, None],
        jnp.stack(input_grads)[:, None],
        query_w_grad,
        key_w_grad,
        value_w_grad,
        outgate_w_grad,
        output_grad.T,
        gate_w_grad,
        up_w_grad,
        down_grad.T,
        gains[:feature_dim],
        gains[feature_dim : 2 * feature_dim],
        gains[2 * feature_dim : 2 * feature_dim + HEAD_SIZE],
        gains[2 * feature_dim + HEAD_SIZE :],
    )


def solution(mesh):
    return jax.shard_map(
        shards,
        mesh=mesh,
        in_specs=(
            P(None, "fsdp", "seq", None),
            P(None, "fsdp", "seq", None),
            P("fsdp", "seq"),
            P("fsdp", "seq"),
            P("fsdp", "seq"),
            P("fsdp", "seq"),
            P("seq", "fsdp"),
            P("fsdp", "seq"),
            P("fsdp", "seq"),
            P("seq", "fsdp"),
            P(),
            P(),
            P(),
            P(),
            P(None, "fsdp", None),
            P(None, "fsdp", None),
        ),
        out_specs=(
            P(None, "fsdp", "seq", None),
            P(None, "fsdp", "seq", None),
            P("fsdp", "seq"),
            P("fsdp", "seq"),
            P("fsdp", "seq"),
            P("fsdp", "seq"),
            P("seq", "fsdp"),
            P("fsdp", "seq"),
            P("fsdp", "seq"),
            P("seq", "fsdp"),
            P(),
            P(),
            P(),
            P(),
        ),
        check_vma=False,
    )
```

time: 2210 us -> 1360 us (0.62)
  waiting for transfers between devices: 1460 us -> 388 us
  local copies, waits for them, and re-layouts: 51.5 us -> 197 us
  starting transfers between devices: 3 us -> 110 us
  other arithmetic: 90 us -> 164 us
  matrix products: 542 us -> 472 us
  blocking collectives: 39.7 us -> 0 us
    reduce_scatter x24 -> x5, waiting for transfers between devices: 924 us -> 0.01 us  [scatter_weight(): lax.psum_scatter(total.astype(jnp.bfloat16), 'fsdp', scatter_dimension=0,...]
    all_gather x16 -> x4, waiting for transfers between devices: 529 us -> 25.4 us  [gather_weight(): return lax.all_gather(shard, 'fsdp', axis=0, tiled=True)]
    ppermute x0 -> x90, waiting for transfers between devices: none -> 362 us  [the longest x8 107 us: gather_tokens(): along = lax.ppermute(own, 'seq', flips(4, 2))]
    ppermute x0 -> x90, starting transfers between devices: none -> 110 us  [the longest x8 12.8 us: gather_tokens(): far_bottom = lax.ppermute(across[half:], 'seq', flips(4, 2))]
    dot_general x32 -> x20, matrix products: 244 us -> 184 us  [the longest x10 93.2 us: outer(): jnp.einsum('rd,rf->df', left, right, preferred_element_type=jnp.float32)]
    psum x1 -> x0, blocking collectives: 39.7 us -> none  [shards(): lax.psum((attn_gain_sum, ffn_gain_sum, query_gain_sum, key_gain_sum), ('s...]
    reshape x0 -> x18, local copies, waits for them, and re-layouts: none -> 38.3 us  [the longest x4 9.53 us: shards(): query_grad_raw.reshape(full_len, query_heads, HEAD_SIZE)]
    mul x0 -> x17, local copies, waits for them, and re-layouts: none -> 22.7 us  [the longest x6 10 us: apply_rotary(): return values * cosine_lookup + turned * sine_lookup]
  transfers between devices with their start and end apart: 40 -> 99, of which waited for: 34 -> 54; matrix products, arithmetic and copies ran while one was open for 25% -> 47% of each run, Pallas kernels for 0% -> 0%
where the time goes in v1:
time: 1360 us; the launch traced here: 1350 us
  matrix products  472 us (35%)
  waiting for transfers between devices  388 us (29%)
  local copies, waits for them, and re-layouts  197 us (14%)
  other arithmetic  164 us (12%)
  starting transfers between devices  110 us (8%)
  between operations  17.5 us (1%)
    ppermute x8, waiting for transfers between devices, gather_tokens(): along = lax.ppermute(own, 'seq', flips(4, 2))  107 us
    dot_general x8, matrix products, dense(): return jnp.dot(left, right, preferred_element_type=jnp.float32)  102 us
    dot_general x10, matrix products, outer(): jnp.einsum('rd,rf->df', left, right, preferred_element_type=jnp.float32)  93.2 us
    dot_general x10, matrix products, times_transposed(): jnp.einsum('re,de->rd', left, right, preferred_element_type=jnp.float32)  90.3 us
    ppermute x8, waiting for transfers between devices, scatter_tokens(): relay_top = lax.ppermute(far_top, 'seq', flips(4, 1))  66.8 us
    dot_general x4, matrix products, attend_backward(): jnp.einsum('hgqk,khd->qhgd', score_grad, key_rows, preferred_element_type...  64.5 us
    dot_general x4, matrix products, attend_backward(): jnp.einsum('hgqk,qhgd->khd', score_grad, query_row_block[begin_row:end_ro...  62.8 us
    ppermute x8, waiting for transfers between devices, gather_tokens(): far_top = lax.ppermute(along[:half], 'seq', flips(4, 1))  53.9 us
  transfers between devices with their start and end apart: 99, of which 54 were waited for; matrix products, arithmetic and copies ran while one was open for 47% of the time, Pallas kernels for 0%

profile of v1, /device:TPU:0, one launch (start us, length us, event | category | flops | bytes accessed | tf_op | source)
XLA Modules:
  0.0 1347.8 jit_solution(7969959453537671113)
XLA Ops:
  31.6 11.3 collective-permute-done.21
  61.7 15.9 %all-gather.5.cloned.1.call-done = bf16[2048,1536]{1,0:T(8,128)(2,1)} async-done(((bf16[256,1536]{1,0:T(8,128)(2,1)}), bf16[2048,1536]{1,0:T(8,128)(2,1)}) %all-gather.5.cloned.1.call-update) | async-done | bytes 6291472 | tf_op jit(solution)/shard_map/all_gather | solution.py:202
  77.7 10.0 fusion.239
  155.1 11.2 collective-permute-done.25
  183.9 19.9 %collective-permute-done.61 = bf16[256,2048]{1,0:T(8,128)(2,1)S(1)} collective-permute-done((bf16[256,2048]{1,0:T(8,128)(2,1)S(1)}, bf16[256,2048]{1,0:T(8,128)(2,1)S(1)}, u32[]{:S(2)}, u32[]{:S(2)}) %collective-permute-start.61) | collective-permute-done | bytes 1048608 | tf_op jit(solution)/shard_map/ppermute | solution.py:146
  220.9 9.4 collective-permute-done.62
  230.4 11.9 collective-permute-done.31
  263.0 18.9 %fusion.240 = f32[1024,3072]{1,0:T(8,128)} fusion(bf16[1024,2048]{1,0:T(8,128)(2,1)} %constant_dynamic-update-slice_fusion.15, bf16[2048,3072]{1,0:T(8,128)(2,1)} %all-gather.9.cloned.1.call-done), kind=kOutput, calls=%fused_computation.485 | convolution fusion | flops 12884901888 | bytes 29360128 | tf_op jit(solution)/shard_map/dot_general | solution.py:133
  281.9 9.4 all-gather.11.cloned.1.call-done
  291.3 16.8 %multiply_convert_fusion.1 = (bf16[1024,1536]{1,0:T(8,128)(2,1)}, bf16[1024,1536]{1,0:T(8,128)(2,1)S(1)}, bf16[1024,1536]{1,0:T(8,128)(2,1)}) fusion(f32[1024,3072]{1,0:T(8,128)} %fusion.240, bf16[1024,2048]{1,0:T(8,128)(2,1)} %copy-done.125, bf16[2048,1536]{0,1:T(8,128)(2,1)} %all-gather.11.cloned.1.call-done), kind=kOutput, calls=%fused_computation.59 | convolution fusion | flops 6466043904 | bytes 32505856 | tf_op jit(solution)/shard_map/dot_general | solution.py:133
  308.1 12.0 fusion.26
  320.1 10.2 add_convert_fusion.4
  334.1 11.3 collective-permute-done.65
  384.0 13.7 %collective-permute-done.1 = bf16[256,2048]{1,0:T(8,128)(2,1)} collective-permute-done((bf16[256,2048]{1,0:T(8,128)(2,1)}, bf16[256,2048]{1,0:T(8,128)(2,1)}, u32[]{:S(2)}, u32[]{:S(2)}) %collective-permute-start.1) | collective-permute-done | bytes 1048608 | tf_op jit(solution)/shard_map/ppermute | solution.py:146
  413.5 10.0 fusion.237
  489.2 10.7 collective-permute-done.5
  505.5 9.4 collective-permute-done.6
  534.1 14.4 %collective-permute-done.41 = bf16[256,2048]{1,0:T(8,128)(2,1)S(1)} collective-permute-done((bf16[256,2048]{1,0:T(8,128)(2,1)S(1)}, bf16[256,2048]{1,0:T(8,128)(2,1)S(1)}, u32[]{:S(2)}, u32[]{:S(2)}) %collective-permute-start.41) | collective-permute-done | bytes 1048608 | tf_op jit(solution)/shard_map/ppermute | solution.py:146
  554.4 24.3 %collective-permute-done.42 = bf16[128,2048]{1,0:T(8,128)(2,1)S(1)} collective-permute-done((bf16[128,2048]{1,0:T(8,128)(2,1)S(1)}, bf16[128,2048]{1,0:T(8,128)(2,1)S(1)}, u32[]{:S(2)}, u32[]{:S(2)}) %collective-permute-start.42) | collective-permute-done | bytes 524320 | tf_op jit(solution)/shard_map/ppermute | solution.py:147
  591.7 15.6 %fusion.238 = f32[1024,3072]{1,0:T(8,128)} fusion(bf16[1024,2048]{1,0:T(8,128)(2,1)S(1)} %constant_dynamic-update-slice_fusion.5, bf16[2048,3072]{1,0:T(8,128)(2,1)S(1)} %bitcast.701), kind=kOutput, calls=%fused_computation.483 | convolution fusion | flops 12884901888 | bytes 29360128 | tf_op jit(solution)/shard_map/dot_general | solution.py:133
  607.3 15.5 %multiply_convert_fusion.3 = (bf16[1024,1536]{1,0:T(8,128)(2,1)}, bf16[1024,1536]{1,0:T(8,128)(2,1)S(1)}, bf16[1024,1536]{1,0:T(8,128)(2,1)}) fusion(f32[1024,3072]{1,0:T(8,128)} %fusion.238, bf16[1024,2048]{1,0:T(8,128)(2,1)S(1)} %constant_dynamic-update-slice_fusion.20, bf16[2048,1536]{0,1:T(8,128)(2,1)} %all-gather.11.cloned.1.call-done), kind=kOutput, calls=%fused_computation.61 | convolution fusion | flops 6466043904 | bytes 32505856 | tf_op jit(solution)/shard_map/dot_general | solution.py:133
  622.8 12.0 fusion.28
  634.8 10.9 add_convert_fusion.5
  693.2 21.9 %collective-permute-done.71 = bf16[256,2048]{1,0:T(8,128)(2,1)S(1)} collective-permute-done((bf16[256,2048]{1,0:T(8,128)(2,1)S(1)}, bf16[256,2048]{1,0:T(8,128)(2,1)S(1)}, u32[]{:S(2)}, u32[]{:S(2)}) %collective-permute-start.71) | collective-permute-done | bytes 1048608 | tf_op jit(solution)/shard_map/ppermute | solution.py:146
  718.8 13.5 collective-permute-done.51
  756.2 10.1 fusion.244
  766.4 9.1 add_convert_fusion
  775.6 10.5 fusion.242
  786.2 9.2 add_convert_fusion.2
  795.4 10.5 convolution_convert_fusion.2
  836.7 11.5 fusion.243
  855.9 9.9 convolution_convert_fusion.3
  873.3 12.1 add_convert_fusion.1
  930.3 14.4 %fusion.137 = f32[2,128,1024]{2,1,0:T(8,128)} fusion(bf16[512,2,2,128]{3,0,2,1:T(8,128)(2,1)S(1)} %bitcast.675, f32[2,1024,512,2]{2,1,3,0:T(8,128)} %fusion.185, f32[2,2,512,1024]{2,3,1,0:T(8,128)} %copy-done.6, f32[2,2,512]{2,1,0:T(2,128)S(1)} %log_add_fusion.3), kind=kOutput, calls=%fused_computation.250 | convolution fusion | flops 551554048 | bytes 18358272 | tf_op jit(solution)/shard_map/hgqk,qhgd->khd/dot_general | solution.py:117
  944.7 14.8 %broadcast_multiply_fusion.3 = (f32[1024,2,128]{0,2,1:T(8,128)}, f32[1024,2,128]{0,2,1:T(8,128)}) fusion(f32[1024,128]{0,1:T(8,128)S(1)} %copy-done.81, f32[2,128,1024]{2,1,0:T(8,128)} %fusion.137, bf16[512,2,2,128]{3,0,2,1:T(8,128)(2,1)S(1)} %bitcast.673, f32[2,1024,512,2]{2,1,3,0:T(8,128)} %fusion.183, f32[2,2,512,1024]{2,3,1,0:T(8,128)} %copy-done.5, ...), kind=kOutput, calls=%fused_computation.337 | convolution fusion | flops 552078336 | bytes 20979712 | tf_op jit(solution)/shard_map/hgqk,qhgd->khd/dot_general | solution.py:117
  968.7 16.4 %fusion.134 = f32[2,128,1024]{2,1,0:T(8,128)} fusion(bf16[512,2,2,128]{3,0,2,1:T(8,128)(2,1)} %bitcast.671, f32[2,1024,512,2]{2,1,3,0:T(8,128)} %fusion.179, f32[2,2,512,1024]{2,3,1,0:T(8,128)} %copy-done.4, f32[2,2,512]{2,1,0:T(2,128)S(1)} %log_add_fusion.1), kind=kOutput, calls=%fused_computation.247 | convolution fusion | flops 551554048 | bytes 18358272 | tf_op jit(solution)/shard_map/hgqk,qhgd->khd/dot_general | solution.py:117
  989.6 17.2 %broadcast_multiply_fusion.2 = (f32[1024,2,128]{0,2,1:T(8,128)}, f32[1024,2,128]{0,2,1:T(8,128)}) fusion(f32[1024,128]{0,1:T(8,128)} %copy-done.79, f32[2,128,1024]{2,1,0:T(8,128)} %fusion.134, bf16[512,2,2,128]{3,0,2,1:T(8,128)(2,1)} %bitcast.668, f32[2,1024,512,2]{2,1,3,0:T(8,128)} %fusion.177, f32[2,2,512,1024]{2,3,1,0:T(8,128)} %copy-done.3, ...), kind=kOutput, calls=%fused_computation.336 | convolution fusion | flops 552078336 | bytes 20979712 | tf_op jit(solution)/shard_map/hgqk,qhgd->khd/dot_general | solution.py:117
  1012.6 16.2 %fusion.59 = f32[2,128,2,512]{3,1,2,0:T(8,128)} fusion(bf16[1024,2,128,1]{0,2,3,1:T(8,128)(2,1)} %copy-done.77, f32[2,1024,512,2]{2,1,3,0:T(8,128)} %fusion.183, f32[2,2,512,1024]{2,3,1,0:T(8,128)} %copy-done.5, f32[2,2,512]{2,1,0:T(2,128)S(1)} %log_add_fusion.2), kind=kOutput, calls=%fused_computation.102 | convolution fusion | flops 551554048 | bytes 18358272 | tf_op jit(solution)/shard_map/hgqk,khd->qhgd/dot_general | solution.py:115
  1028.8 16.3 %fusion.56 = f32[2,128,2,512]{3,1,2,0:T(8,128)} fusion(bf16[1024,2,128,1]{0,2,3,1:T(8,128)(2,1)S(1)} %copy-done.78, f32[2,1024,512,2]{2,1,3,0:T(8,128)} %fusion.185, f32[2,2,512,1024]{2,3,1,0:T(8,128)} %copy-done.6, f32[2,2,512]{2,1,0:T(2,128)S(1)} %log_add_fusion.3), kind=kOutput, calls=%fused_computation.99 | convolution fusion | flops 551554048 | bytes 18358272 | tf_op jit(solution)/shard_map/hgqk,khd->qhgd/dot_general | solution.py:115
  1060.1 15.9 %fusion.65 = f32[2,128,2,512]{3,1,2,0:T(8,128)} fusion(bf16[1024,2,128,1]{0,2,3,1:T(8,128)(2,1)} %copy-done.76, f32[2,1024,512,2]{2,1,3,0:T(8,128)} %fusion.177, f32[2,2,512,1024]{2,3,1,0:T(8,128)} %copy-done.3, f32[2,2,512]{2,1,0:T(2,128)S(1)} %log_add_fusion), kind=kOutput, calls=%fused_computation.108 | convolution fusion | flops 551554048 | bytes 18358272 | tf_op jit(solution)/shard_map/hgqk,khd->qhgd/dot_general | solution.py:115
  1076.0 16.0 %fusion.62 = f32[2,128,2,512]{3,1,2,0:T(8,128)} fusion(bf16[1024,2,128,1]{0,2,3,1:T(8,128)(2,1)} %copy-done.76, f32[2,1024,512,2]{2,1,3,0:T(8,128)} %fusion.179, f32[2,2,512,1024]{2,3,1,0:T(8,128)} %copy-done.4, f32[2,2,512]{2,1,0:T(2,128)S(1)} %log_add_fusion.1), kind=kOutput, calls=%fused_computation.105 | convolution fusion | flops 551554048 | bytes 18358272 | tf_op jit(solution)/shard_map/hgqk,khd->qhgd/dot_general | solution.py:115
  1161.9 8.9 fusion.131
  1183.7 11.8 fusion.172
  1195.5 12.5 add_convert_fusion.3
  1208.1 9.4 convolution_convert_fusion
  1220.6 8.8 convolution_convert_fusion.1
  1240.7 18.0 %collective-permute-done.55 = bf16[128,2048]{1,0:T(8,128)(2,1)S(1)} collective-permute-done((bf16[128,2048]{1,0:T(8,128)(2,1)S(1)}, bf16[128,2048]{1,0:T(8,128)(2,1)S(1)}, u32[]{:S(2)}, u32[]{:S(2)}) %collective-permute-start.55) | collective-permute-done | bytes 524320 | tf_op jit(solution)/shard_map/ppermute | solution.py:167
  1264.3 19.7 %collective-permute-done.54 = bf16[128,2048]{1,0:T(8,128)(2,1)S(1)} collective-permute-done((bf16[128,2048]{1,0:T(8,128)(2,1)S(1)}, bf16[128,2048]{1,0:T(8,128)(2,1)S(1)}, u32[]{:S(2)}, u32[]{:S(2)}) %collective-permute-start.54) | collective-permute-done | bytes 524320 | tf_op jit(solution)/shard_map/ppermute | solution.py:169
  (890 shorter events, 690.9 us)
Async XLA Ops:
  7.2 70.5 %all-gather.5.cloned.1.call-start = ((), (), s32[]{:S(2)}) async-start(), calls=%async_computation.5 | async-start | bytes 7077888 | tf_op jit(solution)/shard_map/all_gather | solution.py:202
  9.5 137.5 %all-gather.7.cloned.1.call-start = ((), (), s32[]{:S(2)}) async-start(), calls=%async_computation.6 | async-start | bytes 2359296 | tf_op jit(solution)/shard_map/all_gather | solution.py:202
  10.3 252.7 %all-gather.9.cloned.1.call-start = ((), (), s32[]{:S(2)}) async-start(), calls=%async_computation.7 | async-start | bytes 14155776 | tf_op jit(solution)/shard_map/all_gather | solution.py:202
  13.0 278.3 %all-gather.11.cloned.1.call-start = ((), (), s32[]{:S(2)}) async-start(), calls=%async_computation.8 | async-start | bytes 7077888 | tf_op jit(solution)/shard_map/all_gather | solution.py:202
  15.0 32.2 %collective-permute-start.20 = (bf16[256,2048]{1,0:T(8,128)(2,1)}, bf16[256,2048]{1,0:T(8,128)(2,1)}, u32[]{:S(2)}, u32[]{:S(2)}) collective-permute-start(bf16[256,2048]{1,0:T(8,128)(2,1)} %get-tuple-element.144), channel_id=1, source_target_pairs={{0,8},{8,0},{16,24},{24,16},{1,9},{9,1},{17,25},{25,17},{2,10},{10... | collective-permute-start | bytes 3145736 | tf_op jit(solution)/shard_map/ppermute | solution.py:145
  18.0 24.9 %collective-permute-start.21 = (bf16[256,2048]{1,0:T(8,128)(2,1)}, bf16[256,2048]{1,0:T(8,128)(2,1)}, u32[]{:S(2)}, u32[]{:S(2)}) collective-permute-start(bf16[256,2048]{1,0:T(8,128)(2,1)} %get-tuple-element.144), channel_id=1, source_target_pairs={{0,16},{8,24},{16,0},{24,8},{1,17},{9,25},{17,1},{25,9},{2,18},{10... | collective-permute-start | bytes 3145736 | tf_op jit(solution)/shard_map/ppermute | solution.py:146
  19.5 1307.7 %reduce-scatter.8.cloned.1.call-start = ((), (), s32[]{:S(2)}) async-start(), calls=%async_computation.10 | async-start | bytes 2359296 | tf_op jit(solution)/shard_map/reduce_scatter | solution.py:206
  153.1 23.8 %collective-permute-start.24 = (bf16[128,2048]{1,0:T(8,128)(2,1)S(1)}, bf16[128,2048]{1,0:T(8,128)(2,1)S(1)}, u32[]{:S(2)}, u32[]{:S(2)}) collective-permute-start(bf16[128,2048]{1,0:T(8,128)(2,1)S(1)} %get-tuple-element.209), channel_id=1, source_target_pairs={{0,8},{8,0},{16,24},{24,16},{1,9},{9,1},{17,25},{25,17},{2,10},{10... | collective-permute-start | bytes 1572872 | tf_op jit(solution)/shard_map/ppermute | solution.py:169
  169.3 34.5 %collective-permute-start.61 = (bf16[256,2048]{1,0:T(8,128)(2,1)S(1)}, bf16[256,2048]{1,0:T(8,128)(2,1)S(1)}, u32[]{:S(2)}, u32[]{:S(2)}) collective-permute-start(bf16[256,2048]{1,0:T(8,128)(2,1)S(1)} %get-tuple-element.220), channel_id=1, source_target_pairs={{0,16},{8,24},{16,0},{24,8},{1,17},{9,25},{17,1},{25,9},{2,18},{10... | collective-permute-start | bytes 3145736 | tf_op jit(solution)/shard_map/ppermute | solution.py:146
  169.8 43.0 %collective-permute-start.27 = (bf16[128,2048]{1,0:T(8,128)(2,1)S(1)}, bf16[128,2048]{1,0:T(8,128)(2,1)S(1)}, u32[]{:S(2)}, u32[]{:S(2)}) collective-permute-start(bf16[128,2048]{1,0:T(8,128)(2,1)S(1)} %get-tuple-element.211), channel_id=1, source_target_pairs={{0,16},{8,24},{16,0},{24,8},{1,17},{9,25},{17,1},{25,9},{2,18},{10... | collective-permute-start | bytes 1572872 | tf_op jit(solution)/shard_map/ppermute | solution.py:170
  181.8 31.0 %collective-permute-start.29 = (bf16[128,2048]{1,0:T(8,128)(2,1)S(1)}, bf16[128,2048]{1,0:T(8,128)(2,1)S(1)}, u32[]{:S(2)}, u32[]{:S(2)}) collective-permute-start(bf16[128,2048]{1,0:T(8,128)(2,1)S(1)} %get-tuple-element.208), channel_id=1, source_target_pairs={{0,8},{8,0},{16,24},{24,16},{1,9},{9,1},{17,25},{25,17},{2,10},{10... | collective-permute-start | bytes 1572872 | tf_op jit(solution)/shard_map/ppermute | solution.py:172
  183.4 35.7 %collective-permute-start.60 = (bf16[256,2048]{1,0:T(8,128)(2,1)S(1)}, bf16[256,2048]{1,0:T(8,128)(2,1)S(1)}, u32[]{:S(2)}, u32[]{:S(2)}) collective-permute-start(bf16[256,2048]{1,0:T(8,128)(2,1)S(1)} %get-tuple-element.220), channel_id=1, source_target_pairs={{0,8},{8,0},{16,24},{24,16},{1,9},{9,1},{17,25},{25,17},{2,10},{10... | collective-permute-start | bytes 3145736 | tf_op jit(solution)/shard_map/ppermute | solution.py:145
  203.9 26.5 %collective-permute-start.62 = (bf16[128,2048]{1,0:T(8,128)(2,1)S(1)}, bf16[128,2048]{1,0:T(8,128)(2,1)S(1)}, u32[]{:S(2)}, u32[]{:S(2)}) collective-permute-start(bf16[128,2048]{1,0:T(8,128)(2,1)S(1)} %slice.676), channel_id=1, source_target_pairs={{0,8},{8,0},{16,24},{24,16},{1,9},{9,1},{17,25},{25,17},{2,10},{10... | collective-permute-start | bytes 1572872 | tf_op jit(solution)/shard_map/ppermute | solution.py:147
  214.8 38.0 %collective-permute-start.30 = (bf16[256,2048]{1,0:T(8,128)(2,1)S(1)}, bf16[256,2048]{1,0:T(8,128)(2,1)S(1)}, u32[]{:S(2)}, u32[]{:S(2)}) collective-permute-start(bf16[256,2048]{1,0:T(8,128)(2,1)S(1)} %get-tuple-element.142), channel_id=1, source_target_pairs={{0,8},{8,0},{16,24},{24,16},{1,9},{9,1},{17,25},{25,17},{2,10},{10... | collective-permute-start | bytes 3145736 | tf_op jit(solution)/shard_map/ppermute | solution.py:145
  216.2 26.0 %collective-permute-start.31 = (bf16[256,2048]{1,0:T(8,128)(2,1)S(1)}, bf16[256,2048]{1,0:T(8,128)(2,1)S(1)}, u32[]{:S(2)}, u32[]{:S(2)}) collective-permute-start(bf16[256,2048]{1,0:T(8,128)(2,1)S(1)} %get-tuple-element.142), channel_id=1, source_target_pairs={{0,16},{8,24},{16,0},{24,8},{1,17},{9,25},{17,1},{25,9},{2,18},{10... | collective-permute-start | bytes 3145736 | tf_op jit(solution)/shard_map/ppermute | solution.py:146
  219.2 31.4 %collective-permute-start.63 = (bf16[128,2048]{1,0:T(8,128)(2,1)S(1)}, bf16[128,2048]{1,0:T(8,128)(2,1)S(1)}, u32[]{:S(2)}, u32[]{:S(2)}) collective-permute-start(bf16[128,2048]{1,0:T(8,128)(2,1)S(1)} %slice.677), channel_id=1, source_target_pairs={{0,16},{8,24},{16,0},{24,8},{1,17},{9,25},{17,1},{25,9},{2,18},{10... | collective-permute-start | bytes 1572872 | tf_op jit(solution)/shard_map/ppermute | solution.py:148
  332.0 23.8 %collective-permute-start.64 = (bf16[128,2048]{1,0:T(8,128)(2,1)S(1)}, bf16[128,2048]{1,0:T(8,128)(2,1)S(1)}, u32[]{:S(2)}, u32[]{:S(2)}) collective-permute-start(bf16[128,2048]{1,0:T(8,128)(2,1)S(1)} %get-tuple-element.197), channel_id=1, source_target_pairs={{0,8},{8,0},{16,24},{24,16},{1,9},{9,1},{17,25},{25,17},{2,10},{10... | collective-permute-start | bytes 1572872 | tf_op jit(solution)/shard_map/ppermute | solution.py:169
  332.6 23.3 %collective-permute-start.68 = (bf16[128,2048]{1,0:T(8,128)(2,1)S(1)}, bf16[128,2048]{1,0:T(8,128)(2,1)S(1)}, u32[]{:S(2)}, u32[]{:S(2)}) collective-permute-start(bf16[128,2048]{1,0:T(8,128)(2,1)S(1)} %get-tuple-element.198), channel_id=1, source_target_pairs={{0,16},{8,24},{16,0},{24,8},{1,17},{9,25},{17,1},{25,9},{2,18},{10... | collective-permute-start | bytes 1572872 | tf_op jit(solution)/shard_map/ppermute | solution.py:168
  374.2 28.0 %collective-permute-start = (bf16[256,2048]{1,0:T(8,128)(2,1)}, bf16[256,2048]{1,0:T(8,128)(2,1)}, u32[]{:S(2)}, u32[]{:S(2)}) collective-permute-start(bf16[256,2048]{1,0:T(8,128)(2,1)} %get-tuple-element.140), channel_id=1, source_target_pairs={{0,8},{8,0},{16,24},{24,16},{1,9},{9,1},{17,25},{25,17},{2,10},{10... | collective-permute-start | bytes 3145736 | tf_op jit(solution)/shard_map/ppermute | solution.py:145
  501.5 24.5 %collective-permute-start.7 = (bf16[128,2048]{1,0:T(8,128)(2,1)S(1)}, bf16[128,2048]{1,0:T(8,128)(2,1)S(1)}, u32[]{:S(2)}, u32[]{:S(2)}) collective-permute-start(bf16[128,2048]{1,0:T(8,128)(2,1)S(1)} %get-tuple-element.193), channel_id=1, source_target_pairs={{0,16},{8,24},{16,0},{24,8},{1,17},{9,25},{17,1},{25,9},{2,18},{10... | collective-permute-start | bytes 1572872 | tf_op jit(solution)/shard_map/ppermute | solution.py:170
  516.8 35.8 %collective-permute-start.40 = (bf16[256,2048]{1,0:T(8,128)(2,1)S(1)}, bf16[256,2048]{1,0:T(8,128)(2,1)S(1)}, u32[]{:S(2)}, u32[]{:S(2)}) collective-permute-start(bf16[256,2048]{1,0:T(8,128)(2,1)S(1)} %copy-done.107), channel_id=1, source_target_pairs={{0,8},{8,0},{16,24},{24,16},{1,9},{9,1},{17,25},{25,17},{2,10},{10... | collective-permute-start | bytes 3145736 | tf_op jit(solution)/shard_map/ppermute | solution.py:145
  517.4 31.2 %collective-permute-start.41 = (bf16[256,2048]{1,0:T(8,128)(2,1)S(1)}, bf16[256,2048]{1,0:T(8,128)(2,1)S(1)}, u32[]{:S(2)}, u32[]{:S(2)}) collective-permute-start(bf16[256,2048]{1,0:T(8,128)(2,1)S(1)} %copy-done.107), channel_id=1, source_target_pairs={{0,16},{8,24},{16,0},{24,8},{1,17},{9,25},{17,1},{25,9},{2,18},{10... | collective-permute-start | bytes 3145736 | tf_op jit(solution)/shard_map/ppermute | solution.py:146
  531.1 47.6 %collective-permute-start.11 = (bf16[256,2048]{1,0:T(8,128)(2,1)S(1)}, bf16[256,2048]{1,0:T(8,128)(2,1)S(1)}, u32[]{:S(2)}, u32[]{:S(2)}) collective-permute-start(bf16[256,2048]{1,0:T(8,128)(2,1)S(1)} %get-tuple-element.138), channel_id=1, source_target_pairs={{0,16},{8,24},{16,0},{24,8},{1,17},{9,25},{17,1},{25,9},{2,18},{10... | collective-permute-start | bytes 3145736 | tf_op jit(solution)/shard_map/ppermute | solution.py:146
  532.7 47.7 %collective-permute-start.10 = (bf16[256,2048]{1,0:T(8,128)(2,1)S(1)}, bf16[256,2048]{1,0:T(8,128)(2,1)S(1)}, u32[]{:S(2)}, u32[]{:S(2)}) collective-permute-start(bf16[256,2048]{1,0:T(8,128)(2,1)S(1)} %get-tuple-element.138), channel_id=1, source_target_pairs={{0,8},{8,0},{16,24},{24,16},{1,9},{9,1},{17,25},{25,17},{2,10},{10... | collective-permute-start | bytes 3145736 | tf_op jit(solution)/shard_map/ppermute | solution.py:145
  548.6 30.1 %collective-permute-start.42 = (bf16[128,2048]{1,0:T(8,128)(2,1)S(1)}, bf16[128,2048]{1,0:T(8,128)(2,1)S(1)}, u32[]{:S(2)}, u32[]{:S(2)}) collective-permute-start(bf16[128,2048]{1,0:T(8,128)(2,1)S(1)} %slice.648), channel_id=1, source_target_pairs={{0,8},{8,0},{16,24},{24,16},{1,9},{9,1},{17,25},{25,17},{2,10},{10... | collective-permute-start | bytes 1572872 | tf_op jit(solution)/shard_map/ppermute | solution.py:147
  552.7 27.7 %collective-permute-start.43 = (bf16[128,2048]{1,0:T(8,128)(2,1)S(1)}, bf16[128,2048]{1,0:T(8,128)(2,1)S(1)}, u32[]{:S(2)}, u32[]{:S(2)}) collective-permute-start(bf16[128,2048]{1,0:T(8,128)(2,1)S(1)} %slice.649), channel_id=1, source_target_pairs={{0,16},{8,24},{16,0},{24,8},{1,17},{9,25},{17,1},{25,9},{2,18},{10... | collective-permute-start | bytes 1572872 | tf_op jit(solution)/shard_map/ppermute | solution.py:148
  688.6 26.5 %collective-permute-start.71 = (bf16[256,2048]{1,0:T(8,128)(2,1)S(1)}, bf16[256,2048]{1,0:T(8,128)(2,1)S(1)}, u32[]{:S(2)}, u32[]{:S(2)}) collective-permute-start(bf16[256,2048]{1,0:T(8,128)(2,1)S(1)} %get-tuple-element.160), channel_id=1, source_target_pairs={{0,16},{8,24},{16,0},{24,8},{1,17},{9,25},{17,1},{25,9},{2,18},{10... | collective-permute-start | bytes 3145736 | tf_op jit(solution)/shard_map/ppermute | solution.py:146
  691.1 26.0 %collective-permute-start.70 = (bf16[256,2048]{1,0:T(8,128)(2,1)S(1)}, bf16[256,2048]{1,0:T(8,128)(2,1)S(1)}, u32[]{:S(2)}, u32[]{:S(2)}) collective-permute-start(bf16[256,2048]{1,0:T(8,128)(2,1)S(1)} %get-tuple-element.160), channel_id=1, source_target_pairs={{0,8},{8,0},{16,24},{24,16},{1,9},{9,1},{17,25},{25,17},{2,10},{10... | collective-permute-start | bytes 3145736 | tf_op jit(solution)/shard_map/ppermute | solution.py:145
  692.5 39.7 %collective-permute-start.51 = (bf16[256,2048]{1,0:T(8,128)(2,1)S(1)}, bf16[256,2048]{1,0:T(8,128)(2,1)S(1)}, u32[]{:S(2)}, u32[]{:S(2)}) collective-permute-start(bf16[256,2048]{1,0:T(8,128)(2,1)S(1)} %get-tuple-element.133), channel_id=1, source_target_pairs={{0,16},{8,24},{16,0},{24,8},{1,17},{9,25},{17,1},{25,9},{2,18},{10... | collective-permute-start | bytes 3145736 | tf_op jit(solution)/shard_map/ppermute | solution.py:146
  692.6 43.8 %collective-permute-start.50 = (bf16[256,2048]{1,0:T(8,128)(2,1)S(1)}, bf16[256,2048]{1,0:T(8,128)(2,1)S(1)}, u32[]{:S(2)}, u32[]{:S(2)}) collective-permute-start(bf16[256,2048]{1,0:T(8,128)(2,1)S(1)} %get-tuple-element.133), channel_id=1, source_target_pairs={{0,8},{8,0},{16,24},{24,16},{1,9},{9,1},{17,25},{25,17},{2,10},{10... | collective-permute-start | bytes 3145736 | tf_op jit(solution)/shard_map/ppermute | solution.py:145
  715.1 26.9 %collective-permute-start.72 = (bf16[128,2048]{1,0:T(8,128)(2,1)S(1)}, bf16[128,2048]{1,0:T(8,128)(2,1)S(1)}, u32[]{:S(2)}, u32[]{:S(2)}) collective-permute-start(bf16[128,2048]{1,0:T(8,128)(2,1)S(1)} %slice.686), channel_id=1, source_target_pairs={{0,8},{8,0},{16,24},{24,16},{1,9},{9,1},{17,25},{25,17},{2,10},{10... | collective-permute-start | bytes 1572872 | tf_op jit(solution)/shard_map/ppermute | solution.py:147
  717.1 24.9 %collective-permute-start.73 = (bf16[128,2048]{1,0:T(8,128)(2,1)S(1)}, bf16[128,2048]{1,0:T(8,128)(2,1)S(1)}, u32[]{:S(2)}, u32[]{:S(2)}) collective-permute-start(bf16[128,2048]{1,0:T(8,128)(2,1)S(1)} %slice.687), channel_id=1, source_target_pairs={{0,16},{8,24},{16,0},{24,8},{1,17},{9,25},{17,1},{25,9},{2,18},{10... | collective-permute-start | bytes 1572872 | tf_op jit(solution)/shard_map/ppermute | solution.py:148
  756.1 573.1 %reduce-scatter.14.cloned.1.call-start = ((), (), s32[]{:S(2)}) async-start(), calls=%async_computation.13 | async-start | bytes 7077888 | tf_op jit(solution)/shard_map/reduce_scatter | solution.py:206
  775.5 556.7 %reduce-scatter.10.cloned.1.call-start = ((), (), s32[]{:S(2)}) async-start(), calls=%async_computation.11 | async-start | bytes 7077888 | tf_op jit(solution)/shard_map/reduce_scatter | solution.py:206
  795.4 539.3 %reduce-scatter.12.cloned.1.call-start = ((), (), s32[]{:S(2)}) async-start(), calls=%async_computation.12 | async-start | bytes 7077888 | tf_op jit(solution)/shard_map/reduce_scatter | solution.py:206
  808.5 23.3 %collective-permute-start.34 = (bf16[128,2048]{1,0:T(8,128)(2,1)}, bf16[128,2048]{1,0:T(8,128)(2,1)}, u32[]{:S(2)}, u32[]{:S(2)}) collective-permute-start(bf16[128,2048]{1,0:T(8,128)(2,1)} %get-tuple-element.203), channel_id=1, source_target_pairs={{0,8},{8,0},{16,24},{24,16},{1,9},{9,1},{17,25},{25,17},{2,10},{10... | collective-permute-start | bytes 1572872 | tf_op jit(solution)/shard_map/ppermute | solution.py:169
  869.7 364.2 %collective-permute-start.14 = (bf16[128,2048]{1,0:T(8,128)(2,1)}, bf16[128,2048]{1,0:T(8,128)(2,1)}, u32[]{:S(2)}, u32[]{:S(2)}) collective-permute-start(bf16[128,2048]{1,0:T(8,128)(2,1)} %get-tuple-element.185), channel_id=1, source_target_pairs={{0,8},{8,0},{16,24},{24,16},{1,9},{9,1},{17,25},{25,17},{2,10},{10... | collective-permute-start | bytes 1572872 | tf_op jit(solution)/shard_map/ppermute | solution.py:169
  871.3 363.5 %collective-permute-start.18 = (bf16[128,2048]{1,0:T(8,128)(2,1)}, bf16[128,2048]{1,0:T(8,128)(2,1)}, u32[]{:S(2)}, u32[]{:S(2)}) collective-permute-start(bf16[128,2048]{1,0:T(8,128)(2,1)} %get-tuple-element.186), channel_id=1, source_target_pairs={{0,16},{8,24},{16,0},{24,8},{1,17},{9,25},{17,1},{25,9},{2,18},{10... | collective-permute-start | bytes 1572872 | tf_op jit(solution)/shard_map/ppermute | solution.py:168
  872.4 416.0 %collective-permute-start.17 = (bf16[128,2048]{1,0:T(8,128)(2,1)}, bf16[128,2048]{1,0:T(8,128)(2,1)}, u32[]{:S(2)}, u32[]{:S(2)}) collective-permute-start(bf16[128,2048]{1,0:T(8,128)(2,1)} %get-tuple-element.187), channel_id=1, source_target_pairs={{0,16},{8,24},{16,0},{24,8},{1,17},{9,25},{17,1},{25,9},{2,18},{10... | collective-permute-start | bytes 1572872 | tf_op jit(solution)/shard_map/ppermute | solution.py:170
  885.4 451.7 %reduce-scatter.6.cloned.1.call-start = ((), (), s32[]{:S(2)}) async-start(), calls=%async_computation.9 | async-start | bytes 7077888 | tf_op jit(solution)/shard_map/reduce_scatter | solution.py:206
  887.7 348.3 %collective-permute-start.16 = (bf16[128,2048]{1,0:T(8,128)(2,1)}, bf16[128,2048]{1,0:T(8,128)(2,1)}, u32[]{:S(2)}, u32[]{:S(2)}) collective-permute-start(bf16[128,2048]{1,0:T(8,128)(2,1)} %add_convert_fusion.22), channel_id=1, source_target_pairs={{0,16},{8,24},{16,0},{24,8},{1,17},{9,25},{17,1},{25,9},{2,18},{10... | collective-permute-start | bytes 1572872 | tf_op jit(solution)/shard_map/ppermute | solution.py:171
  1233.4 26.1 %collective-permute-start.74 = (bf16[128,2048]{1,0:T(8,128)(2,1)S(1)}, bf16[128,2048]{1,0:T(8,128)(2,1)S(1)}, u32[]{:S(2)}, u32[]{:S(2)}) collective-permute-start(bf16[128,2048]{1,0:T(8,128)(2,1)S(1)} %get-tuple-element.173), channel_id=1, source_target_pairs={{0,8},{8,0},{16,24},{24,16},{1,9},{9,1},{17,25},{25,17},{2,10},{10... | collective-permute-start | bytes 1572872 | tf_op jit(solution)/shard_map/ppermute | solution.py:169
  1234.0 27.0 %collective-permute-start.78 = (bf16[128,2048]{1,0:T(8,128)(2,1)S(1)}, bf16[128,2048]{1,0:T(8,128)(2,1)S(1)}, u32[]{:S(2)}, u32[]{:S(2)}) collective-permute-start(bf16[128,2048]{1,0:T(8,128)(2,1)S(1)} %get-tuple-element.174), channel_id=1, source_target_pairs={{0,16},{8,24},{16,0},{24,8},{1,17},{9,25},{17,1},{25,9},{2,18},{10... | collective-permute-start | bytes 1572872 | tf_op jit(solution)/shard_map/ppermute | solution.py:168
  1234.7 24.0 %collective-permute-start.55 = (bf16[128,2048]{1,0:T(8,128)(2,1)S(1)}, bf16[128,2048]{1,0:T(8,128)(2,1)S(1)}, u32[]{:S(2)}, u32[]{:S(2)}) collective-permute-start(bf16[128,2048]{1,0:T(8,128)(2,1)S(1)} %get-tuple-element.170), channel_id=1, source_target_pairs={{0,8},{8,0},{16,24},{24,16},{1,9},{9,1},{17,25},{25,17},{2,10},{10... | collective-permute-start | bytes 1572872 | tf_op jit(solution)/shard_map/ppermute | solution.py:167
  1236.0 25.0 %collective-permute-start.76 = (bf16[128,2048]{1,0:T(8,128)(2,1)S(1)}, bf16[128,2048]{1,0:T(8,128)(2,1)S(1)}, u32[]{:S(2)}, u32[]{:S(2)}) collective-permute-start(bf16[128,2048]{1,0:T(8,128)(2,1)S(1)} %add_convert_fusion.10), channel_id=1, source_target_pairs={{0,16},{8,24},{16,0},{24,8},{1,17},{9,25},{17,1},{25,9},{2,18},{10... | collective-permute-start | bytes 1572872 | tf_op jit(solution)/shard_map/ppermute | solution.py:171
  1258.8 31.0 %collective-permute-start.19 = (bf16[128,2048]{1,0:T(8,128)(2,1)S(1)}, bf16[128,2048]{1,0:T(8,128)(2,1)S(1)}, u32[]{:S(2)}, u32[]{:S(2)}) collective-permute-start(bf16[128,2048]{1,0:T(8,128)(2,1)S(1)} %get-tuple-element.184), channel_id=1, source_target_pairs={{0,8},{8,0},{16,24},{24,16},{1,9},{9,1},{17,25},{25,17},{2,10},{10... | collective-permute-start | bytes 1572872 | tf_op jit(solution)/shard_map/ppermute | solution.py:172
  1259.4 24.5 %collective-permute-start.54 = (bf16[128,2048]{1,0:T(8,128)(2,1)S(1)}, bf16[128,2048]{1,0:T(8,128)(2,1)S(1)}, u32[]{:S(2)}, u32[]{:S(2)}) collective-permute-start(bf16[128,2048]{1,0:T(8,128)(2,1)S(1)} %get-tuple-element.167), channel_id=1, source_target_pairs={{0,8},{8,0},{16,24},{24,16},{1,9},{9,1},{17,25},{25,17},{2,10},{10... | collective-permute-start | bytes 1572872 | tf_op jit(solution)/shard_map/ppermute | solution.py:169
  1261.0 25.0 %collective-permute-start.56 = (bf16[128,2048]{1,0:T(8,128)(2,1)S(1)}, bf16[128,2048]{1,0:T(8,128)(2,1)S(1)}, u32[]{:S(2)}, u32[]{:S(2)}) collective-permute-start(bf16[128,2048]{1,0:T(8,128)(2,1)S(1)} %add_convert_fusion.14), channel_id=1, source_target_pairs={{0,16},{8,24},{16,0},{24,8},{1,17},{9,25},{17,1},{25,9},{2,18},{10... | collective-permute-start | bytes 1572872 | tf_op jit(solution)/shard_map/ppermute | solution.py:171
  (243 other events, 3384.4 us)
Sparse Core Ops, SparseCore 0:
  10.2 67.4 all-gather.4
  79.3 29.2 all-gather.6
  110.8 115.7 all-gather.8
  228.0 63.3 all-gather.10
  756.3 34.3 reduce-scatter.7
  792.8 68.4 reduce-scatter.13
  863.6 68.1 reduce-scatter.9
  934.1 68.1 reduce-scatter.11
  1208.2 67.1 reduce-scatter.5
